TPU v7x, 256 devices: a 4x2x16 block of a 4x16x16 slice. The times are simulated.
256 devices in a mesh: groups: 2 (over y), gx: 128 (over z, x, core).
Axes of the slice: x: 4, y: 2, z: 16, core: 2. Of those that a mesh axis runs over, the one named last changes fastest.
The devices are a block of a 4x16x16 slice.
Arguments:
- stream_in: bfloat16 [256, 8192], P(('groups', 'gx')), parts along dimension 0, may hold values from -6 to 6
- query: bfloat16 [256, 8192], P(('groups', 'gx')), parts along dimension 0, may hold values from -4.5 to 4.5
- key_new: bfloat16 [256, 1024], P(('groups', 'gx')), parts along dimension 0, may hold values from -4.5 to 4.5
- value_new: bfloat16 [256, 1024], P(('groups', 'gx')), parts along dimension 0, may hold values from -6 to 6
- key_cache: bfloat16 [256, 128, 1024], P(('groups', 'gx')), parts along dimension 0, may hold values from -6 to 6
- value_cache: bfloat16 [256, 128, 1024], P(('groups', 'gx')), parts along dimension 0, may hold values from -6 to 6
- lengths: int32 [256], P(('groups', 'gx')), parts along dimension 0, may hold values from 1 to 128, as said below
- route_ids: int32 [256, 2], P(('groups', 'gx')), parts along dimension 0, may hold values from 0 to 3, as said below
- route_scores: float32 [256, 2], P(('groups', 'gx')), parts along dimension 0, may hold values from -6 to 6
- out_weight: bfloat16 [8192, 8192], P(None, 'gx'), may hold values from -0.0625 to 0.0625
- norm_gain: float32 [8192], replicated, may hold values from 0.1 to 1.9
- gate_weight: bfloat16 [2, 131072, 896], P(None, 'gx'), may hold values from -0.0625 to 0.0625
- up_weight: bfloat16 [2, 131072, 896], P(None, 'gx'), may hold values from -0.0625 to 0.0625
- down_weight: bfloat16 [2, 114688, 1024], P(None, 'gx'), may hold values from -0.046875 to 0.046875
Outputs:
- layer_out: bfloat16 [256, 8192], P(('groups', 'gx')), parts along dimension 0
There are 2 independent parts, one for each index of `groups`. A program takes and returns all parts, laid end to end along the dimension named above; an argument that names none is the same for every part. Nothing has to cross between parts.
Inputs may be any that keep to these rules, and one draw needn't show every extreme that they name: `lengths`: 1 to 128; some sequence fills all 128 slots. `route_ids`: each row names two different experts of 0 to 3; in one replica's batch each of the experts 0 and 1 is named by at most 80 sequences, and one of them by exactly 80.
All inputs are finite; a program needn't handle non-finite values.
Results may differ from a plain program's by a relative error of at most 0.0095.
Values may be sent and summed in bfloat16 or wider, within the bound.
A program may use at most 64 MiB of HBM per device.

v0:
```python
import jax
import jax.numpy as jnp
from jax import lax
from jax.sharding import Mesh
from jax.sharding import PartitionSpec as P

NH = 64
KVH = 8
HS = 128
RESIDENT = 2
MSPLIT = 8
GX = ("gx_0", "gx_1", "gx_2")
GROUPS_GX = ("groups", "gx_0", "gx_1", "gx_2")


def laid_out(blocks, dim):
    lengths = list(blocks.shape[1:])
    lengths[dim] *= blocks.shape[0]
    return jnp.moveaxis(blocks, 0, dim).reshape(lengths)


def all_blocks(value, axes, turns):
    blocks = value
    for k in turns:
        blocks = lax.all_gather(blocks, axes[k])
    done = turns[::-1]
    back = [done.index(k) for k in range(len(axes))]
    blocks = blocks.transpose(*back, *range(len(axes), blocks.ndim))
    return blocks.reshape(-1, *value.shape)


def whole_of(value, axes, turns, dim):
    return laid_out(all_blocks(value, axes, turns), dim)


def in_blocks(value, dim, length):
    lengths = value.shape
    blocks = value.reshape(*lengths[:dim], length, lengths[dim] // length, *lengths[dim + 1 :])
    return jnp.moveaxis(blocks, dim, 0)


def turned_blocks(blocks, axes, turns):
    inside = blocks.shape[1:]
    out = blocks.reshape(*(lax.axis_size(a) for a in axes), *inside)
    for k in turns:
        out = lax.all_to_all(out, axes[k], k, k, tiled=True)
    return out.reshape(-1, *inside)


def exchange_by_chip(value, groups, turns, split_dim, concat_dim):
    length = lax.axis_size(groups[0]) * lax.axis_size(groups[1])
    blocks = in_blocks(value, split_dim, length)
    return laid_out(turned_blocks(blocks, groups, turns), concat_dim)


def side_by_side(arrays, axis, split_dim, concat_dim, along):
    widths = [a.shape[along] for a in arrays]
    both = jnp.concatenate(arrays, axis=along)
    out = lax.all_to_all(both, axis, split_axis=split_dim, concat_axis=concat_dim, tiled=True)
    return tuple(jnp.split(out, [sum(widths[:k]) for k in range(1, len(widths))], axis=along))


def partner(value, axis, distance):
    return lax.ppermute(value, axis, [(i, i ^ 1 << distance) for i in range(lax.axis_size(axis))])


def attend_local(query, key_new, value_new, key_cache, value_cache, lengths):
    seqs = query.shape[0]
    slots = key_cache.shape[1]
    group = NH // KVH
    scale = HS ** (-0.5)
    q_four = query.reshape(seqs, KVH, group, HS)
    k_all = key_cache.reshape(seqs, slots, KVH, HS)
    v_all = value_cache.reshape(seqs, slots, KVH, HS)
    k_own = key_new.reshape(seqs, KVH, HS)
    v_own = value_new.reshape(seqs, KVH, HS)
    scores = (
        jnp.einsum("skgd,sckd->skgc", q_four, k_all, preferred_element_type=jnp.float32) * scale
    )
    live = jnp.arange(slots, dtype=jnp.int32)[None, :] < lengths[:, None]
    scores = jnp.where(live[:, None, None, :], scores, -1e30)
    own = jnp.einsum("skgd,skd->skg", q_four, k_own, preferred_element_type=jnp.float32) * scale
    top = jnp.maximum(jnp.max(scores, axis=-1), own)
    e_cache = jnp.exp(scores - top[..., None])
    e_own = jnp.exp(own - top)
    total = jnp.sum(e_cache, axis=-1) + e_own
    p_cache = (e_cache / total[..., None]).astype(jnp.bfloat16)
    p_own = (e_own / total).astype(jnp.bfloat16)
    mixed = jnp.einsum("skgc,sckd->skgd", p_cache, v_all, preferred_element_type=jnp.float32)
    mixed = mixed + p_own.astype(jnp.float32)[..., None] * v_own.astype(jnp.float32)[:, :, None, :]
    return mixed.reshape(seqs, NH * HS).astype(jnp.bfloat16)


def gated(parts):
    return (jax.nn.silu(parts[..., 0, :]) * parts[..., 1, :]).astype(jnp.bfloat16)


def on_device(
    stream_in,
    query,
    key_new,
    value_new,
    key_cache,
    value_cache,
    lengths,
    route_ids,
    route_scores,
    out_weight,
    norm_gain,
    gate_weight,
    up_weight,
    down_weight,
):
    seqs = stream_in.shape[0]
    width = stream_in.shape[1]
    members = lax.axis_size(GX)
    batch = seqs * members
    hsplit = members // MSPLIT
    low_bits = hsplit.bit_length() - 1
    model_bits = MSPLIT.bit_length() - 1
    place = lax.axis_index(GX)
    model_block = place // hsplit
    block_width = width // MSPLIT
    hidden_cols = gate_weight.shape[2]
    narrow = hidden_cols // MSPLIT
    attn = attend_local(query, key_new, value_new, key_cache, value_cache, lengths)
    proj_cols = jnp.dot(
        whole_of(attn, GX, (1, 0, 2), 0), out_weight, preferred_element_type=jnp.float32
    ).astype(jnp.bfloat16)
    proj = exchange_by_chip(proj_cols, (("gx_0", "gx_1"), "gx_2"), (1, 0), 0, 1)
    resid = stream_in.astype(jnp.float32) + proj.astype(jnp.float32)
    power = jnp.mean(resid * resid, axis=-1, keepdims=True)
    normed = (resid * lax.rsqrt(power + 1e-05) * norm_gain).astype(jnp.bfloat16)
    probs = jax.nn.softmax(route_scores, axis=-1)
    columns = []
    for expert in range(RESIDENT):
        columns.append(jnp.sum(jnp.where(route_ids == expert, probs, 0.0), axis=-1))
    weight = jnp.stack(columns, axis=-1).astype(jnp.bfloat16)
    spread = normed.reshape(seqs, MSPLIT, block_width).transpose(1, 0, 2)
    spread = jnp.broadcast_to(spread[:, None], (MSPLIT, hsplit, seqs, block_width)).reshape(
        members, seqs, block_width
    )
    copies = jnp.broadcast_to(weight[None], (members, seqs, RESIDENT))
    rows_in, weight_in = side_by_side((spread, copies), GX, 0, 0, 2)
    rows_in = rows_in.reshape(batch, block_width)
    weight_all = weight_in.reshape(batch, RESIDENT)
    gate_view = gate_weight.reshape(RESIDENT, block_width, MSPLIT, narrow)
    up_view = up_weight.reshape(RESIDENT, block_width, MSPLIT, narrow)
    gate_part = jnp.einsum("bd,rdpc->bprc", rows_in, gate_view, preferred_element_type=jnp.float32)
    up_part = jnp.einsum("bd,rdpc->bprc", rows_in, up_view, preferred_element_type=jnp.float32)
    parts = jnp.stack([gate_part, up_part], axis=3)
    for bit in reversed(range(model_bits)):
        half = parts.shape[1] // 2
        lower = parts[:, :half]
        upper = parts[:, half:]
        mine_high = model_block >> bit & 1 == 1
        keep = jnp.where(mine_high, upper, lower)
        other = jnp.where(mine_high, lower, upper)
        parts = keep + partner(other.astype(jnp.bfloat16), GX, low_bits + bit).astype(other.dtype)
    share = gated(parts)
    for bit in range(model_bits):
        other = partner(share, GX, low_bits + bit)
        mine_high = model_block >> bit & 1 == 1
        share = jnp.where(
            mine_high,
            jnp.concatenate([other, share], axis=1),
            jnp.concatenate([share, other], axis=1),
        )
    down_view = down_weight.reshape(RESIDENT, MSPLIT, narrow, block_width)
    scales = weight_all.astype(jnp.float32)
    result = jnp.zeros((batch, block_width), jnp.float32)
    for expert in range(RESIDENT):
        term = jnp.einsum(
            "bpc,pcn->bn",
            share[:, :, expert],
            down_view[expert],
            preferred_element_type=jnp.float32,
        )
        result = result + scales[:, expert][:, None] * term
    partial_out = result.reshape(members, seqs, block_width)
    got = lax.all_to_all(
        partial_out.astype(jnp.bfloat16), GX, split_axis=0, concat_axis=0, tiled=True
    ).astype(partial_out.dtype)
    got = jnp.sum(got.reshape(MSPLIT, hsplit, seqs, block_width), axis=1)
    ffn = got.transpose(1, 0, 2).reshape(seqs, width)
    return (resid + ffn).astype(jnp.bfloat16)


def solution(mesh):
    finer = Mesh(
        mesh.devices.reshape(mesh.shape["groups"], 16, 4, 2), ("groups", "gx_0", "gx_1", "gx_2")
    )
    in_specs = (
        P(GROUPS_GX, None),
        P(GROUPS_GX, None),
        P(GROUPS_GX, None),
        P(GROUPS_GX, None),
        P(GROUPS_GX, None, None),
        P(GROUPS_GX, None, None),
        P(GROUPS_GX),
        P(GROUPS_GX, None),
        P(GROUPS_GX, None),
        P(None, GX),
        P(),
        P(None, GX, None),
        P(None, GX, None),
        P(None, GX, None),
    )
    out_specs = P(GROUPS_GX, None)
    return jax.shard_map(
        on_device, mesh=finer, in_specs=in_specs, out_specs=out_specs, check_vma=False
    )
```

profile of v0, /device:TPU:33, one launch (start us, length us, event | category | flops | bytes accessed | tf_op | source)
XLA Modules:
  0.0 391.5 jit_solution(17718389902913505557)
XLA Ops:
  7.3 0.7 convert_element_type.138
  8.0 1.0 copy.59
  9.0 0.9 reduce.10
  9.8 0.8 fusion.15
  10.7 0.3 fusion.27
  11.0 0.2 fusion.14
  11.2 1.0 copy.60
  12.2 0.2 fusion.6
  12.4 11.3 %all_gather.16 = bf16[4,1,8192]{2,1,0:T(2,128)(2,1)} all-gather(bf16[1,1,8192]{2,1,0:T(2,128)(2,1)S(1)} %convert_element_type.121), channel_id=1, replica_groups=mesh['groups'=2,'gx_0'=16,'gx_1'=4,'gx_2'=2] {'gx_1'}, dimensions={0}, use_global_device_ids=true | all-gather | bytes 81920 | tf_op jit(solution)/shard_map/all_gather | solution.py:25
  23.9 77.3 %all-gather.5.cloned.1.call-done = bf16[64,1,8192]{2,1,0:T(2,128)(2,1)} async-done(((bf16[4,1,8192]{2,1,0:T(2,128)(2,1)}), bf16[64,1,8192]{2,1,0:T(2,128)(2,1)}) %all-gather.5.cloned.1.call-update) | async-done | bytes 1048592 | tf_op jit(solution)/shard_map/all_gather | solution.py:25
  101.2 7.9 %reduce.11 = bf16[64,8192]{1,0:T(8,128)(2,1)S(1)} reduce(bf16[64,1,8192]{2,1,0:T(2,128)(2,1)} %all-gather.5.cloned.1.call-done, bf16[]{:T(256)} %constant.67), dimensions={1}, to_apply=%all-gather.reduce_sub_computation | reduce | bytes 2097154 | tf_op jit(solution)/shard_map/all_gather | solution.py:25
  109.1 1.2 reshape.269
  110.4 0.6 reduce_max.19
  111.0 1.3 fusion.25
  112.3 2.0 fusion.23
  114.3 23.7 %all-gather.7.cloned.1.call-done = bf16[32,4,1,8192]{3,1,2,0:T(4,128)(2,1)} async-done(((bf16[16,4,1,8192]{3,1,2,0:T(4,128)(2,1)}), bf16[32,4,1,8192]{3,1,2,0:T(4,128)(2,1)}) %all-gather.7.cloned.1.call-update) | async-done | bytes 2097168 | tf_op jit(solution)/shard_map/all_gather | solution.py:25
  138.0 3.8 copy.73
  141.8 2.2 reshape_reshape.6
  144.0 2.4 convolution_convert_fusion
  146.5 0.1 copy.45
  146.7 3.6 all_to_all.20
  150.4 0.7 copy.47
  151.1 16.3 %all-to-all-start.1 = ((bf16[64,2,1,64]{3,1,2,0:T(2,128)(2,1)}), bf16[64,2,1,64]{3,1,2,0:T(2,128)(2,1)S(1)}, u32[]{:S(2)}, u32[]{:S(2)}) async-start(bf16[64,2,1,64]{3,1,2,0:T(2,128)(2,1)} %copy.47), calls=%async_computation.1 | async-start | bytes 65536 | tf_op jit(solution)/shard_map/all_to_all | solution.py:46
  167.4 1.2 pad_maximum_fusion.2
  168.6 11.2 %all-to-all-done.1 = bf16[64,2,1,64]{3,1,2,0:T(2,128)(2,1)S(1)} async-done(((bf16[64,2,1,64]{3,1,2,0:T(2,128)(2,1)}), bf16[64,2,1,64]{3,1,2,0:T(2,128)(2,1)S(1)}, u32[]{:S(2)}, u32[]{:S(2)}) %all-to-all-start.1) | async-done | bytes 16416 | tf_op jit(solution)/shard_map/all_to_all | solution.py:46
  179.8 0.1 reshape.265
  179.9 0.7 multiply_reduce_fusion
  181.3 0.1 convert_reduce_fusion
  181.5 0.5 broadcast.69
  182.0 0.8 reduce.18
  182.8 1.1 reshape.288
  183.9 8.8 %all-to-all-start.2 = ((bf16[128,2,513]{2,1,0:T(2,128)(2,1)}), bf16[128,2,513]{2,1,0:T(2,128)(2,1)S(1)}, u32[]{:S(2)}, u32[]{:S(2)}) async-start(bf16[128,2,513]{2,1,0:T(2,128)(2,1)} %reshape.288), calls=%async_computation.2 | async-start | bytes 655360 | tf_op jit(solution)/shard_map/all_to_all | solution.py:59
  192.7 6.1 %copy.50 = bf16[2,1024,896]{1,2,0:T(8,128)(2,1)} copy(bf16[2,1024,896]{2,1,0:T(8,128)(2,1)} %param.25) | data formatting | bytes 7340032 | tf_op args[11]
  198.8 6.1 %copy.51 = bf16[2,1024,896]{1,2,0:T(8,128)(2,1)} copy(bf16[2,1024,896]{2,1,0:T(8,128)(2,1)} %param.26) | data formatting | bytes 7340032 | tf_op args[12]
  204.9 10.4 %all-to-all-done.2 = bf16[128,2,513]{2,1,0:T(2,128)(2,1)S(1)} async-done(((bf16[128,2,513]{2,1,0:T(2,128)(2,1)}), bf16[128,2,513]{2,1,0:T(2,128)(2,1)S(1)}, u32[]{:S(2)}, u32[]{:S(2)}) %all-to-all-start.2) | async-done | bytes 262688 | tf_op jit(solution)/shard_map/all_to_all | solution.py:59
  215.3 0.5 reshape.289
  215.9 0.5 split.9
  216.4 3.3 fusion.13
  219.7 1.1 fusion.12
  220.9 0.9 select_convert_fusion
  221.8 3.8 collective-permute-start
  225.5 23.0 %collective-permute-done = bf16[128,4,2,2,112]{0,4,1,2,3:T(8,128)(2,1)} collective-permute-done((bf16[128,4,2,2,112]{0,4,1,2,3:T(8,128)(2,1)}, bf16[128,4,2,2,112]{0,4,1,2,3:T(8,128)(2,1)}, u32[]{:S(2)}, u32[]{:S(2)}) %collective-permute-start) | collective-permute-done | bytes 458784 | tf_op jit(solution)/shard_map/ppermute | solution.py:64
  248.5 1.1 convert_add_fusion
  249.7 0.9 copy-done.2
  250.6 26.9 %collective-permute-start.1 = (bf16[128,2,2,2,112]{0,4,1,2,3:T(8,128)(2,1)S(1)}, bf16[128,2,2,2,112]{0,4,1,2,3:T(8,128)(2,1)S(1)}, u32[]{:S(2)}, u32[]{:S(2)}) collective-permute-start(bf16[128,2,2,2,112]{0,4,1,2,3:T(8,128)(2,1)S(1)} %select_convert_fusion.1), channel_id=1, source_target_pairs={{0,32},{1,33},{2,34},{3,35},{4,36},{5,37},{6,38},{7,39},{8,40},{9,... | collective-permute-start | bytes 688136 | tf_op jit(solution)/shard_map/ppermute | solution.py:64
  277.6 19.4 %collective-permute-done.1 = bf16[128,2,2,2,112]{0,4,1,2,3:T(8,128)(2,1)S(1)} collective-permute-done((bf16[128,2,2,2,112]{0,4,1,2,3:T(8,128)(2,1)S(1)}, bf16[128,2,2,2,112]{0,4,1,2,3:T(8,128)(2,1)S(1)}, u32[]{:S(2)}, u32[]{:S(2)}) %collective-permute-start.1) | collective-permute-done | bytes 229408 | tf_op jit(solution)/shard_map/ppermute | solution.py:64
  296.9 1.2 convert_add_fusion.1
  298.2 0.1 collective-permute-start.2
  298.3 5.9 %collective-permute-done.2 = bf16[128,1,2,2,112]{0,4,1,2,3:T(8,128)(2,1)S(1)} collective-permute-done((bf16[128,1,2,2,112]{0,4,1,2,3:T(8,128)(2,1)S(1)}, bf16[128,1,2,2,112]{0,4,1,2,3:T(8,128)(2,1)S(1)}, u32[]{:S(2)}, u32[]{:S(2)}) %collective-permute-start.2) | collective-permute-done | bytes 114720 | tf_op jit(solution)/shard_map/ppermute | solution.py:64
  304.3 0.4 collective-permute-start.3
  304.7 3.9 collective-permute-done.3
  308.6 1.8 collective-permute-start.4
  310.4 2.4 fusion.26
  312.8 8.7 %collective-permute-done.4 = bf16[128,2,2,112]{0,3,2,1:T(8,128)(2,1)S(1)} collective-permute-done((bf16[128,2,2,112]{0,3,2,1:T(8,128)(2,1)S(1)}, bf16[128,2,2,112]{0,3,2,1:T(8,128)(2,1)S(1)}, u32[]{:S(2)}, u32[]{:S(2)}) %collective-permute-start.4) | collective-permute-done | bytes 114720 | tf_op jit(solution)/shard_map/ppermute | solution.py:64
  321.5 4.1 %collective-permute-start.5 = (bf16[128,4,2,112]{0,3,2,1:T(8,128)(2,1)S(1)}, bf16[128,4,2,112]{0,3,2,1:T(8,128)(2,1)S(1)}, u32[]{:S(2)}, u32[]{:S(2)}) collective-permute-start(bf16[128,4,2,112]{0,3,2,1:T(8,128)(2,1)S(1)} %maximum_select_fusion.1), channel_id=1, source_target_pairs={{0,64},{1,65},{2,66},{3,67},{4,68},{5,69},{6,70},{7,71},{8,72},{9,... | collective-permute-start | bytes 688136 | tf_op jit(solution)/shard_map/ppermute | solution.py:64
  325.7 0.2 slice_reduce_fusion.1
  325.9 23.0 %collective-permute-done.5 = bf16[128,4,2,112]{0,3,2,1:T(8,128)(2,1)S(1)} collective-permute-done((bf16[128,4,2,112]{0,3,2,1:T(8,128)(2,1)S(1)}, bf16[128,4,2,112]{0,3,2,1:T(8,128)(2,1)S(1)}, u32[]{:S(2)}, u32[]{:S(2)}) %collective-permute-start.5) | collective-permute-done | bytes 229408 | tf_op jit(solution)/shard_map/ppermute | solution.py:64
  348.9 0.5 fusion
  349.4 0.5 fusion.4
  349.9 0.8 reduce.19
  350.7 0.2 reshape.290
  350.9 32.7 %all_to_all.21 = bf16[128,2,512]{2,1,0:T(2,128)(2,1)S(1)} all-to-all(bf16[128,2,512]{2,1,0:T(2,128)(2,1)S(1)} %reshape.290), channel_id=1, replica_groups=mesh['groups'=2,'gx_0'=16,'gx_1'=4,'gx_2'=2] {'gx_0','gx_1','gx_2'}, dimensions={0} | all-to-all | bytes 524288 | tf_op jit(solution)/shard_map/all_to_all | solution.py:181
  383.5 0.2 reshape.291
  384.0 0.7 add_convert_fusion
  (38 shorter events, 1.1 us)
Async XLA Ops:
  6.5 137.5 %copy-start = (bf16[8192,64]{0,1:T(8,128)(2,1)S(1)}, bf16[8192,64]{0,1:T(8,128)(2,1)}, u32[]{:S(2)}) copy-start(bf16[8192,64]{0,1:T(8,128)(2,1)} %param.23) | copy-start | bytes 3145732
  6.6 94.6 %all-gather.5.cloned.1.call-start = ((), (), s32[]{:S(2)}) async-start(), calls=%async_computation.4 | async-start | bytes 2228224 | tf_op jit(solution)/shard_map/all_gather | solution.py:25
  23.8 114.2 %all-gather.7.cloned.1.call-start = ((), (), s32[]{:S(2)}) async-start(), calls=%async_computation.5 | async-start | bytes 3145728 | tf_op jit(solution)/shard_map/all_gather | solution.py:25
  109.1 1.3 copy-start.6
  109.1 3.3 copy-start.5
  144.0 35.9 %copy-start.3 = (bf16[1,8192]{1,0:T(2,128)(2,1)S(1)}, bf16[1,8192]{1,0:T(2,128)(2,1)}, u32[]{:S(2)}) copy-start(bf16[1,8192]{1,0:T(2,128)(2,1)} %param.14) | copy-start | bytes 49156
  144.0 37.3 %copy-start.4 = (f32[8192]{0:T(1024)S(1)}, f32[8192]{0:T(1024)}, u32[]{:S(2)}) copy-start(f32[8192]{0:T(1024)} %param.24) | copy-start | bytes 98308
  151.1 28.7 %all-to-all-start.1 = ((bf16[64,2,1,64]{3,1,2,0:T(2,128)(2,1)}), bf16[64,2,1,64]{3,1,2,0:T(2,128)(2,1)S(1)}, u32[]{:S(2)}, u32[]{:S(2)}) async-start(bf16[64,2,1,64]{3,1,2,0:T(2,128)(2,1)} %copy.47), calls=%async_computation.1 | async-start | bytes 65536 | tf_op jit(solution)/shard_map/all_to_all | solution.py:46
  183.9 31.5 %all-to-all-start.2 = ((bf16[128,2,513]{2,1,0:T(2,128)(2,1)}), bf16[128,2,513]{2,1,0:T(2,128)(2,1)S(1)}, u32[]{:S(2)}, u32[]{:S(2)}) async-start(bf16[128,2,513]{2,1,0:T(2,128)(2,1)} %reshape.288), calls=%async_computation.2 | async-start | bytes 655360 | tf_op jit(solution)/shard_map/all_to_all | solution.py:59
  216.4 3.3 copy-start.1
  221.8 26.7 %collective-permute-start = (bf16[128,4,2,2,112]{0,4,1,2,3:T(8,128)(2,1)}, bf16[128,4,2,2,112]{0,4,1,2,3:T(8,128)(2,1)}, u32[]{:S(2)}, u32[]{:S(2)}) collective-permute-start(bf16[128,4,2,2,112]{0,4,1,2,3:T(8,128)(2,1)} %select_convert_fusion), channel_id=1, source_target_pairs={{0,64},{1,65},{2,66},{3,67},{4,68},{5,69},{6,70},{7,71},{8,72},{9,... | collective-permute-start | bytes 1376264 | tf_op jit(solution)/shard_map/ppermute | solution.py:64
  249.6 0.9 copy-start.2
  250.6 46.3 %collective-permute-start.1 = (bf16[128,2,2,2,112]{0,4,1,2,3:T(8,128)(2,1)S(1)}, bf16[128,2,2,2,112]{0,4,1,2,3:T(8,128)(2,1)S(1)}, u32[]{:S(2)}, u32[]{:S(2)}) collective-permute-start(bf16[128,2,2,2,112]{0,4,1,2,3:T(8,128)(2,1)S(1)} %select_convert_fusion.1), channel_id=1, source_target_pairs={{0,32},{1,33},{2,34},{3,35},{4,36},{5,37},{6,38},{7,39},{8,40},{9,... | collective-permute-start | bytes 688136 | tf_op jit(solution)/shard_map/ppermute | solution.py:64
  298.2 6.0 %collective-permute-start.2 = (bf16[128,1,2,2,112]{0,4,1,2,3:T(8,128)(2,1)S(1)}, bf16[128,1,2,2,112]{0,4,1,2,3:T(8,128)(2,1)S(1)}, u32[]{:S(2)}, u32[]{:S(2)}) collective-permute-start(bf16[128,1,2,2,112]{0,4,1,2,3:T(8,128)(2,1)S(1)} %select_convert_fusion.2), channel_id=1, source_target_pairs={{0,16},{1,17},{2,18},{3,19},{4,20},{5,21},{6,22},{7,23},{8,24},{9,... | collective-permute-start | bytes 344072 | tf_op jit(solution)/shard_map/ppermute | solution.py:64
  304.3 4.3 %collective-permute-start.3 = (bf16[128,1,2,112]{0,3,2,1:T(8,128)(2,1)S(1)}, bf16[128,1,2,112]{0,3,2,1:T(8,128)(2,1)S(1)}, u32[]{:S(2)}, u32[]{:S(2)}) collective-permute-start(bf16[128,1,2,112]{0,3,2,1:T(8,128)(2,1)S(1)} %fusion.11), channel_id=1, source_target_pairs={{0,16},{1,17},{2,18},{3,19},{4,20},{5,21},{6,22},{7,23},{8,24},{9,... | collective-permute-start | bytes 172040 | tf_op jit(solution)/shard_map/ppermute | solution.py:64
  308.6 12.9 %collective-permute-start.4 = (bf16[128,2,2,112]{0,3,2,1:T(8,128)(2,1)S(1)}, bf16[128,2,2,112]{0,3,2,1:T(8,128)(2,1)S(1)}, u32[]{:S(2)}, u32[]{:S(2)}) collective-permute-start(bf16[128,2,2,112]{0,3,2,1:T(8,128)(2,1)S(1)} %maximum_select_fusion.2), channel_id=1, source_target_pairs={{0,32},{1,33},{2,34},{3,35},{4,36},{5,37},{6,38},{7,39},{8,40},{9,... | collective-permute-start | bytes 344072 | tf_op jit(solution)/shard_map/ppermute | solution.py:64
  321.5 27.4 %collective-permute-start.5 = (bf16[128,4,2,112]{0,3,2,1:T(8,128)(2,1)S(1)}, bf16[128,4,2,112]{0,3,2,1:T(8,128)(2,1)S(1)}, u32[]{:S(2)}, u32[]{:S(2)}) collective-permute-start(bf16[128,4,2,112]{0,3,2,1:T(8,128)(2,1)S(1)} %maximum_select_fusion.1), channel_id=1, source_target_pairs={{0,64},{1,65},{2,66},{3,67},{4,68},{5,69},{6,70},{7,71},{8,72},{9,... | collective-permute-start | bytes 688136 | tf_op jit(solution)/shard_map/ppermute | solution.py:64
Sparse Core Ops, SparseCore 0:
  23.9 77.1 all-gather.4
  110.5 27.4 all-gather.6
where the time goes:
time: 392 us
  waiting for transfers between devices  206 us (53%)
  starting transfers between devices  62.3 us (16%)
  blocking collectives  47.6 us (12%)
  local copies, waits for them, and re-layouts  29.3 us (7%)
  other arithmetic  21.5 us (5%)
  between operations  15.2 us (4%)
  matrix products  9.18 us (2%)
    all_gather x2, waiting for transfers between devices, all_blocks(): blocks = lax.all_gather(blocks, axes[k])  101 us
    ppermute x6, waiting for transfers between devices, partner(): lax.ppermute(value, axis, [(i, i ^ 1 << distance) for i in range(lax.axis...  83.8 us
    ppermute x6, starting transfers between devices, partner(): lax.ppermute(value, axis, [(i, i ^ 1 << distance) for i in range(lax.axis...  37.1 us
    all_to_all x1, blocking collectives, on_device(): lax.all_to_all(partial_out.astype(jnp.bfloat16), GX, split_axis=0, concat...  32.7 us
    unnamed x26, local copies, waits for them, and re-layouts  17.5 us
    all_to_all x1, starting transfers between devices, turned_blocks(): out = lax.all_to_all(out, axes[k], k, k, tiled=True)  16.3 us
    all_gather x1, blocking collectives, all_blocks(): blocks = lax.all_gather(blocks, axes[k])  11.3 us
    all_to_all x1, waiting for transfers between devices, turned_blocks(): out = lax.all_to_all(out, axes[k], k, k, tiled=True)  11.2 us
  transfers between devices with their start and end apart: 10, of which 10 were waited for; matrix products, arithmetic and copies ran while one was open for 5% of the time, Pallas kernels for 0%

commit v1 on v0

v1 whole, which is shorter than its diff:
```python
import functools

import jax
import jax.numpy as jnp
from jax import lax
from jax.experimental import pallas as pl
from jax.experimental.pallas import tpu as pltpu
from jax.sharding import PartitionSpec as P

NH = 64
KVH = 8
HS = 128
RESIDENT = 2
MSPLIT = 8
PLANE = 8
LANES = 128
BF16 = jnp.bfloat16
F32 = jnp.float32
MESH = pl.DeviceIdType.MESH


def nt_dot(a, b):
    return lax.dot_general(a, b, (((1,), (1,)), ((), ())), preferred_element_type=F32)


def nn_dot(a, b):
    return lax.dot_general(a, b, (((1,), (0,)), ((), ())), preferred_element_type=F32)


def copy_to(src, dst, send, recv, target):
    return pltpu.make_async_remote_copy(
        src_ref=src,
        dst_ref=dst,
        send_sem=send,
        recv_sem=recv,
        device_id={"gx": target},
        device_id_type=MESH,
    )


def wait_bytes(ref, sem):
    pltpu.make_async_copy(ref, ref, sem).wait()


def each(count, body, start=0):
    def step(i, carry):
        body(i)
        return carry

    lax.fori_loop(start, count, step, 0)


def layer_kernel(
    cfg,
    lengths,
    route_ids,
    route_scores,
    stream_in,
    query,
    key_new,
    value_new,
    gain,
    key_cache,
    value_cache,
    out_weight,
    gate_weight,
    up_weight,
    down_weight,
    out_ref,
    kbuf,
    vbuf,
    gbuf,
    ubuf,
    dwbuf,
    wbuf,
    qf,
    sf,
    sblk,
    att,
    abuf,
    af,
    pbuf,
    dbuf,
    sbuf,
    meta_out,
    meta_in,
    meta_blk,
    meta_all,
    resid_ref,
    yblk,
    xbuf,
    ssq_row,
    ssq_all,
    xcs,
    own,
    rs_send,
    rs_recv,
    hbuf,
    kout,
    kin,
    lf,
    lout,
    lbuf,
    loc_sem,
    one_send,
    one_recv,
    st_send,
    st_recv,
    me_send,
    me_recv,
    rs_sem,
    ag_sem,
    l_send,
    l_recv,
):
    n = cfg["n"]
    hsplit = n // MSPLIT
    planes = n // PLANE
    batch = n
    width = cfg["width"]
    bw = width // MSPLIT
    pieces = cfg["hidden"] // LANES
    per = cfg["per"]
    pad = cfg["pad"]
    quarters = MSPLIT // RESIDENT
    rows = quarters * pad

    me = lax.axis_index("gx")
    z = me // PLANE
    k = lax.rem(me, PLANE)
    m = me // hsplit
    h = lax.rem(me, hsplit)
    low = me - m * hsplit
    sgn = 1 - 2 * lax.rem(me, 2)

    barrier = pltpu.get_barrier_semaphore()

    def greet(i):
        pl.semaphore_signal(
            barrier, inc=1, device_id={"gx": lax.rem(me + i, n)}, device_id_type=MESH
        )

    each(n, greet, 1)

    loads = [
        pltpu.make_async_copy(key_cache, kbuf, loc_sem.at[0]),
        pltpu.make_async_copy(value_cache, vbuf, loc_sem.at[1]),
        pltpu.make_async_copy(gate_weight, gbuf, loc_sem.at[2]),
        pltpu.make_async_copy(up_weight, ubuf, loc_sem.at[3]),
        pltpu.make_async_copy(down_weight, dwbuf, loc_sem.at[4]),
        pltpu.make_async_copy(
            out_weight.at[:, pl.ds(pl.multiple_of(k * bw, bw), bw)], wbuf.at[k], loc_sem.at[5]
        ),
    ]
    for load in loads:
        load.start()

    for j in range(width // LANES):
        cols = slice(j * LANES, (j + 1) * LANES)
        qf[j : j + 1, :] = query[0:1, cols].astype(F32)
        sf[j : j + 1, :] = stream_in[0:1, cols].astype(F32)
    sblk[...] = sf[...].reshape(MSPLIT, 8, LANES).astype(BF16)

    lane = lax.broadcasted_iota(jnp.int32, (1, LANES), 1)
    s0 = jnp.full((1, LANES), route_scores[0, 0], F32)
    s1 = jnp.full((1, LANES), route_scores[0, 1], F32)
    top = jnp.maximum(s0, s1)
    e0 = jnp.exp(s0 - top)
    e1 = jnp.exp(s1 - top)
    q0 = e0 / (e0 + e1)
    q1 = e1 / (e0 + e1)
    id0 = jnp.full((1, LANES), route_ids[0, 0], jnp.int32)
    id1 = jnp.full((1, LANES), route_ids[0, 1], jnp.int32)
    meta = jnp.zeros((1, LANES), F32)
    for e in range(RESIDENT):
        w = jnp.where(id0 == e, q0, 0.0) + jnp.where(id1 == e, q1, 0.0)
        w = w.astype(BF16).astype(F32)
        picked = jnp.where((id0 == e) | (id1 == e), 1.0, 0.0)
        meta = jnp.where(lane == e, w, meta)
        meta = jnp.where(lane == RESIDENT + e, picked, meta)
    meta_out[...] = meta

    loads[0].wait()
    loads[1].wait()
    scale = HS ** (-0.5)
    slots = kbuf.shape[0]
    live = lax.broadcasted_iota(jnp.int32, (NH // KVH, slots), 1) < lengths[0]
    for g in range(KVH):
        cols = slice(g * HS, (g + 1) * HS)
        q_g = qf[g * 8 : (g + 1) * 8, :]
        k_own = key_new[0:1, cols].astype(F32)
        v_own = value_new[0:1, cols].astype(F32)
        s = nt_dot(q_g.astype(BF16), kbuf[:, cols]) * scale
        s = jnp.where(live, s, -1e30)
        o = jnp.sum(q_g * k_own, axis=1, keepdims=True) * scale
        t = jnp.maximum(jnp.max(s, axis=1, keepdims=True), o)
        es = jnp.exp(s - t)
        eo = jnp.exp(o - t)
        total = jnp.sum(es, axis=1, keepdims=True) + eo
        p = (es / total).astype(BF16)
        po = (eo / total).astype(BF16).astype(F32)
        att[g] = (nn_dot(p, vbuf[:, cols]) + po * v_own).astype(BF16)

    pl.semaphore_wait(barrier, n - 1)

    def plane_send(i):
        j = lax.rem(k + i, PLANE)
        copy_to(
            att.at[j], abuf.at[z, k], one_send.at[0], one_recv.at[0], z * PLANE + j
        ).start()

    each(PLANE, plane_send, 1)

    def w_send(i):
        j = lax.rem(k + i, PLANE)
        copy_to(
            out_weight.at[:, pl.ds(pl.multiple_of(j * bw, bw), bw)],
            wbuf.at[k],
            one_send.at[1],
            one_recv.at[1],
            z * PLANE + j,
        ).start()

    each(PLANE, w_send, 1)

    def stream_send(j):
        target = j * hsplit + z

        @pl.when(target != me)
        def _():
            copy_to(sblk.at[j], sbuf.at[k], st_send.at[j], st_recv.at[k], target).start()
            copy_to(meta_out, meta_in.at[k], me_send.at[j], me_recv.at[k], target).start()

    each(MSPLIT, stream_send)

    @pl.when(z == h)
    def _():
        sbuf[k] = sblk[m]
        meta_in[k] = meta_out[...]

    abuf[z, k] = att[k]
    wait_bytes(abuf.at[0, pl.ds(0, PLANE - 1)], one_recv.at[0])

    def z_send(i):
        target = lax.rem(z + i, planes)
        copy_to(
            abuf.at[z], abuf.at[z], one_send.at[2], one_recv.at[2], target * PLANE + k
        ).start()

    each(planes, z_send, 1)

    def stream_recv(i):
        source = h * PLANE + i

        @pl.when(source != me)
        def _():
            wait_bytes(sbuf.at[i], st_recv.at[i])
            wait_bytes(meta_in.at[i], me_recv.at[i])

    each(PLANE, stream_recv)

    loads[5].wait()
    wait_bytes(wbuf.at[pl.ds(0, PLANE - 1)], one_recv.at[1])
    wait_bytes(abuf.at[pl.ds(0, planes - 1)], one_recv.at[2])

    af[...] = abuf[...].reshape(batch * 8, LANES).astype(F32)
    a = jnp.concatenate(
        [af[pl.ds(j, batch, stride=8), :] for j in range(8)], axis=1
    ).astype(BF16)
    part = nt_dot(a, wbuf[...].reshape(PLANE * wbuf.shape[1], bw))
    pbuf[...] = part.astype(BF16).reshape(hsplit, 8, part.shape[1])

    def proj_send(i):
        j = lax.rem(h + i, hsplit)
        copy_to(pbuf.at[j], dbuf.at[h], one_send.at[3], one_recv.at[3], m * hsplit + j).start()

    each(hsplit, proj_send, 1)
    dbuf[h] = pbuf[h]

    lf[...] = sbuf[...].reshape(PLANE * 8, LANES).astype(F32)
    stream = jnp.concatenate([lf[pl.ds(c, 8, stride=8), :] for c in range(8)], axis=1)
    g8 = gain[pl.ds(pl.multiple_of(m * 8, 8), 8), :]
    gain_row = jnp.concatenate([g8[c : c + 1, :] for c in range(8)], axis=1)
    route = jnp.concatenate([meta_in[i] for i in range(PLANE)], axis=0)

    wait_bytes(dbuf.at[pl.ds(0, hsplit - 1)], one_recv.at[3])
    halves = []
    for half in range(hsplit // PLANE):
        acc = dbuf[half * PLANE].astype(F32)
        for j in range(1, PLANE):
            acc = acc + dbuf[half * PLANE + j].astype(F32)
        halves.append(acc)
    proj = jnp.concatenate(halves, axis=1).astype(BF16).astype(F32)
    resid = stream + proj
    resid_ref[...] = resid
    ssq = jnp.sum(resid * resid, axis=1, keepdims=True)
    lane8 = lax.broadcasted_iota(jnp.int32, (8, LANES), 1)
    meta_blk[...] = jnp.where(lane8 == 2 * RESIDENT, ssq, route)
    meta_all[h] = meta_blk[...]
    yblk[...] = (resid * gain_row).astype(BF16)
    xbuf[h] = yblk[...]

    def spread(i):
        target = m * hsplit + lax.rem(h + i, hsplit)
        copy_to(meta_blk, meta_all.at[h], one_send.at[4], one_recv.at[4], target).start()
        copy_to(yblk, xbuf.at[h], one_send.at[5], one_recv.at[5], target).start()

    each(hsplit, spread, 1)
    wait_bytes(meta_all.at[pl.ds(0, hsplit - 1)], one_recv.at[4])

    info = meta_all[...].reshape(batch, LANES)
    info_t = info.T
    ia = lax.broadcasted_iota(jnp.int32, (batch, batch), 0)
    ib = lax.broadcasted_iota(jnp.int32, (batch, batch), 1)
    before_t = jnp.where(ia < ib, 1.0, 0.0).astype(BF16)
    before = jnp.where(ib < ia, 1.0, 0.0).astype(BF16)
    ranks_t = nn_dot(info_t[0:8].astype(BF16), before_t)
    ranks = nn_dot(before, info.astype(BF16))

    def place_of(rank, picked):
        out = rank
        for c in range(1, quarters):
            out = out + jnp.where(rank >= float(c * per), float(pad - per), 0.0)
        return jnp.where(picked > 0.5, out, -1.0)

    rows_i = [place_of(ranks_t[RESIDENT + e : RESIDENT + e + 1], info_t[RESIDENT + e : RESIDENT + e + 1]) for e in range(RESIDENT)]
    cols_i = [place_of(ranks[:, RESIDENT + e : RESIDENT + e + 1], info[:, RESIDENT + e : RESIDENT + e + 1]) for e in range(RESIDENT)]
    ssq_row[...] = info_t[2 * RESIDENT : 2 * RESIDENT + 1]
    ssq_all[m] = ssq_row[...]

    def ssq_send(i):
        j = lax.rem(m + i, MSPLIT)
        copy_to(ssq_row, ssq_all.at[m], one_send.at[6], one_recv.at[6], j * hsplit + low).start()

    each(MSPLIT, ssq_send, 1)

    wait_bytes(xbuf.at[pl.ds(0, hsplit - 1)], one_recv.at[5])
    x = xbuf[...].reshape(batch, bw)
    r_iota = lax.broadcasted_iota(jnp.int32, (rows, batch), 0).astype(F32)
    for e in range(RESIDENT):
        pick = jnp.where(r_iota == rows_i[e], 1.0, 0.0).astype(BF16)
        xcs[e] = nn_dot(pick, x).astype(BF16)
    loads[2].wait()
    loads[3].wait()

    fwd = MSPLIT // 2
    bwd = MSPLIT - 1 - fwd

    def ring(step):
        return lax.rem(m + sgn * step + 2 * MSPLIT, MSPLIT)

    next_dev = ring(1) * hsplit + low
    prev_dev = ring(-1) * hsplit + low

    def rs_copy(slot, q, target):
        return copy_to(
            rs_send.at[slot, q], rs_recv.at[slot, q], one_send.at[7], rs_sem.at[slot, q], target
        )

    def first(q):
        cols = pl.ds(pl.multiple_of(q * LANES, LANES), LANES)
        for e in range(RESIDENT):
            rhs = jnp.concatenate([gbuf[e, :, cols], ubuf[e, :, cols]], axis=1)
            r = nn_dot(xcs[e], rhs)
            own[q, e * quarters : (e + 1) * quarters] = r.reshape(quarters, pad, 2 * LANES)
        rs_send[0, q] = own[q, ring(fwd)].astype(BF16)
        rs_copy(0, q, next_dev).start()
        rs_send[fwd, q] = own[q, ring(-bwd)].astype(BF16)
        rs_copy(fwd, q, prev_dev).start()

    each(pieces, first)

    for t in range(1, fwd):

        def onward(q, t=t):
            wait_bytes(rs_recv.at[t - 1, q], rs_sem.at[t - 1, q])
            v = rs_recv[t - 1, q].astype(F32) + own[q, ring(fwd - t)]
            rs_send[t, q] = v.astype(BF16)
            rs_copy(t, q, next_dev).start()
            if t < bwd:
                b = fwd + t
                wait_bytes(rs_recv.at[b - 1, q], rs_sem.at[b - 1, q])
                v = rs_recv[b - 1, q].astype(F32) + own[q, ring(t - bwd)]
                rs_send[b, q] = v.astype(BF16)
                rs_copy(b, q, prev_dev).start()

        each(pieces, onward)

    wait_bytes(ssq_all.at[pl.ds(0, MSPLIT - 1)], one_recv.at[6])
    power = ssq_all[0]
    for j in range(1, MSPLIT):
        power = power + ssq_all[j]
    chunk_row = jnp.where(m < quarters, rows_i[0], rows_i[1])
    c_iota = lax.broadcasted_iota(jnp.int32, (pad, batch), 0) + lax.rem(m, quarters) * pad
    hit = c_iota.astype(F32) == chunk_row
    mean = jnp.sum(jnp.where(hit, power, 0.0), axis=1, keepdims=True) / float(width)
    factor = lax.rsqrt(mean + 1e-05)

    def ag_copy(slot, q, chunk, target):
        return copy_to(
            hbuf.at[q, chunk], hbuf.at[q, chunk], one_send.at[8], ag_sem.at[slot, q], target
        )

    def finish(q):
        wait_bytes(rs_recv.at[fwd - 1, q], rs_sem.at[fwd - 1, q])
        wait_bytes(rs_recv.at[MSPLIT - 2, q], rs_sem.at[MSPLIT - 2, q])
        v = own[q, m] + rs_recv[fwd - 1, q].astype(F32) + rs_recv[MSPLIT - 2, q].astype(F32)
        v = v * factor
        ga = v[:, :LANES]
        up = v[:, LANES:]
        hbuf[q, m] = (ga / (1.0 + jnp.exp(-ga)) * up).astype(BF16)
        ag_copy(0, q, m, next_dev).start()
        ag_copy(fwd, q, m, prev_dev).start()

    each(pieces, finish)

    for t in range(1, fwd):

        def relay(q, t=t):
            wait_bytes(hbuf.at[q, ring(-t)], ag_sem.at[t - 1, q])
            ag_copy(t, q, ring(-t), next_dev).start()
            if t < bwd:
                b = fwd + t
                wait_bytes(hbuf.at[q, ring(t)], ag_sem.at[b - 1, q])
                ag_copy(b, q, ring(t), prev_dev).start()

        each(pieces, relay)

    def arrived(q):
        wait_bytes(hbuf.at[q, ring(-fwd)], ag_sem.at[fwd - 1, q])
        wait_bytes(hbuf.at[q, ring(bwd)], ag_sem.at[MSPLIT - 2, q])

    each(pieces, arrived)

    loads[4].wait()
    col_iota = lax.broadcasted_iota(jnp.int32, (batch, rows), 1).astype(F32)
    spreads = []
    for e in range(RESIDENT):
        hc = jnp.concatenate(
            [hbuf[q, e * quarters : (e + 1) * quarters].reshape(rows, LANES) for q in range(pieces)],
            axis=1,
        )
        pick = jnp.where(col_iota == cols_i[e], 1.0, 0.0).astype(BF16)
        spreads.append(nn_dot(pick, hc).astype(BF16))
    tile = 256
    for c in range(bw // tile):
        cols = slice(c * tile, (c + 1) * tile)
        total = jnp.zeros((batch, tile), F32)
        for e in range(RESIDENT):
            total = total + info[:, e : e + 1] * nn_dot(spreads[e], dwbuf[e, :, cols])
        kout[:, :, cols] = total.astype(BF16).reshape(hsplit, 8, tile)

    def ffn_send(i):
        j = lax.rem(h + i, hsplit)
        copy_to(kout.at[j], kin.at[h], one_send.at[9], one_recv.at[7], m * hsplit + j).start()

    each(hsplit, ffn_send, 1)
    kin[h] = kout[h]
    wait_bytes(kin.at[pl.ds(0, hsplit - 1)], one_recv.at[7])
    ffn = kin[0].astype(F32)
    for j in range(1, hsplit):
        ffn = ffn + kin[j].astype(F32)
    final = resid_ref[...] + ffn
    for c in range(8):
        lf[pl.ds(c, 8, stride=8), :] = final[:, c * LANES : (c + 1) * LANES]
    lout[...] = lf[...].reshape(PLANE, 8, LANES).astype(BF16)

    def row_send(i):
        target = h * PLANE + i

        @pl.when(target != me)
        def _():
            copy_to(lout.at[i], lbuf.at[m], l_send.at[i], l_recv.at[m], target).start()

    each(PLANE, row_send)

    @pl.when(z == h)
    def _():
        lbuf[m] = lout[k]

    wait_bytes(abuf.at[0, pl.ds(0, PLANE - 1)], one_send.at[0])
    wait_bytes(wbuf.at[pl.ds(0, PLANE - 1)], one_send.at[1])
    wait_bytes(abuf.at[pl.ds(0, planes - 1)], one_send.at[2])
    wait_bytes(dbuf.at[pl.ds(0, hsplit - 1)], one_send.at[3])
    wait_bytes(meta_all.at[pl.ds(0, hsplit - 1)], one_send.at[4])
    wait_bytes(xbuf.at[pl.ds(0, hsplit - 1)], one_send.at[5])
    wait_bytes(ssq_all.at[pl.ds(0, MSPLIT - 1)], one_send.at[6])
    wait_bytes(rs_send, one_send.at[7])
    wait_bytes(hbuf.at[:, pl.ds(0, MSPLIT - 1)], one_send.at[8])
    wait_bytes(kin.at[pl.ds(0, hsplit - 1)], one_send.at[9])

    def drain(j):
        @pl.when(j * hsplit + z != me)
        def _():
            wait_bytes(sblk.at[j], st_send.at[j])
            wait_bytes(meta_out, me_send.at[j])
            wait_bytes(lbuf.at[j], l_recv.at[j])

        @pl.when(h * PLANE + j != me)
        def _():
            wait_bytes(lout.at[j], l_send.at[j])

    each(MSPLIT, drain)

    qf[...] = lbuf[...].reshape(MSPLIT * 8, LANES).astype(F32)
    for j in range(width // LANES):
        out_ref[0:1, j * LANES : (j + 1) * LANES] = qf[j : j + 1, :].astype(BF16)


def on_device(
    stream_in,
    query,
    key_new,
    value_new,
    key_cache,
    value_cache,
    lengths,
    route_ids,
    route_scores,
    out_weight,
    norm_gain,
    gate_weight,
    up_weight,
    down_weight,
):
    n = lax.axis_size("gx")
    width = stream_in.shape[1]
    slots = key_cache.shape[1]
    kv = key_cache.shape[2]
    hidden = gate_weight.shape[2]
    bw = width // MSPLIT
    hsplit = n // MSPLIT
    planes = n // PLANE
    cols = out_weight.shape[1]
    quarters = MSPLIT // RESIDENT
    per = -(-(5 * n // 8) // quarters)
    pad = -(-per // 8) * 8
    pieces = hidden // LANES
    cfg = dict(n=n, width=width, hidden=hidden, per=per, pad=pad)
    hops = MSPLIT - 1

    def vmem(*shape, dtype=BF16):
        return pltpu.VMEM(shape, dtype)

    scratch = [
        vmem(slots, kv),
        vmem(slots, kv),
        vmem(*gate_weight.shape),
        vmem(*up_weight.shape),
        vmem(*down_weight.shape),
        vmem(PLANE, cols, bw),
        vmem(width // LANES, LANES, dtype=F32),
        vmem(width // LANES, LANES, dtype=F32),
        vmem(MSPLIT, 8, LANES),
        vmem(KVH, 8, HS),
        vmem(planes, PLANE, 8, HS),
        vmem(n * 8, LANES, dtype=F32),
        vmem(hsplit, 8, PLANE * cols),
        vmem(hsplit, 8, PLANE * cols),
        vmem(PLANE, 8, LANES),
        vmem(1, LANES, dtype=F32),
        vmem(PLANE, 1, LANES, dtype=F32),
        vmem(8, LANES, dtype=F32),
        vmem(hsplit, 8, LANES, dtype=F32),
        vmem(8, bw, dtype=F32),
        vmem(8, bw),
        vmem(hsplit, 8, bw),
        vmem(1, LANES, dtype=F32),
        vmem(MSPLIT, 1, LANES, dtype=F32),
        vmem(RESIDENT, quarters * pad, bw),
        vmem(pieces, MSPLIT, pad, 2 * LANES, dtype=F32),
        vmem(hops, pieces, pad, 2 * LANES),
        vmem(hops, pieces, pad, 2 * LANES),
        vmem(pieces, MSPLIT, pad, LANES),
        vmem(hsplit, 8, bw),
        vmem(hsplit, 8, bw),
        vmem(PLANE * 8, LANES, dtype=F32),
        vmem(PLANE, 8, LANES),
        vmem(MSPLIT, 8, LANES),
        pltpu.SemaphoreType.DMA((6,)),
        pltpu.SemaphoreType.DMA((10,)),
        pltpu.SemaphoreType.DMA((8,)),
        pltpu.SemaphoreType.DMA((MSPLIT,)),
        pltpu.SemaphoreType.DMA((PLANE,)),
        pltpu.SemaphoreType.DMA((MSPLIT,)),
        pltpu.SemaphoreType.DMA((PLANE,)),
        pltpu.SemaphoreType.DMA((hops, pieces)),
        pltpu.SemaphoreType.DMA((hops, pieces)),
        pltpu.SemaphoreType.DMA((PLANE,)),
        pltpu.SemaphoreType.DMA((MSPLIT,)),
    ]
    smem = pl.BlockSpec(memory_space=pltpu.SMEM)
    local = pl.BlockSpec(memory_space=pltpu.VMEM)
    anywhere = pl.BlockSpec(memory_space=pl.ANY)
    return pl.pallas_call(
        functools.partial(layer_kernel, cfg),
        out_shape=jax.ShapeDtypeStruct((1, width), BF16),
        in_specs=[smem] * 3 + [local] * 5 + [anywhere] * 6,
        out_specs=local,
        scratch_shapes=scratch,
        compiler_params=pltpu.CompilerParams(
            collective_id=0, has_side_effects=True, vmem_limit_bytes=60 * 1024 * 1024
        ),
        name="layer",
    )(
        lengths,
        route_ids,
        route_scores,
        stream_in,
        query,
        key_new,
        value_new,
        norm_gain.reshape(width // LANES, LANES),
        key_cache.reshape(slots, kv),
        value_cache.reshape(slots, kv),
        out_weight.T,
        gate_weight,
        up_weight,
        down_weight,
    )


def solution(mesh):
    rows = P(("groups", "gx"), None)
    in_specs = (
        rows,
        rows,
        rows,
        rows,
        P(("groups", "gx"), None, None),
        P(("groups", "gx"), None, None),
        P(("groups", "gx")),
        rows,
        rows,
        P(None, "gx"),
        P(),
        P(None, "gx", None),
        P(None, "gx", None),
        P(None, "gx", None),
    )
    return jax.shard_map(
        on_device, mesh=mesh, in_specs=in_specs, out_specs=rows, check_vma=False
    )
```

time: 392 us -> 120 us (0.31)
  waiting for transfers between devices: 206 us -> 0 us
  Pallas kernels: 0 us -> 118 us
  starting transfers between devices: 62.3 us -> 0 us
  blocking collectives: 47.6 us -> 0 us
  local copies, waits for them, and re-layouts: 29.3 us -> 1.41 us
  other arithmetic: 21.5 us -> 0 us
  between operations: 15.2 us -> 0.66 us
  matrix products: 9.18 us -> 0 us
    pallas_call x0 -> x1, Pallas kernels: none -> 118 us  [on_device(): pl.pallas_call(functools.partial(layer_kernel, cfg), out_shape=jax.ShapeD...]
    all_gather x2 -> x0, waiting for transfers between devices: 101 us -> none  [all_blocks(): blocks = lax.all_gather(blocks, axes[k])]
    ppermute x6 -> x0, waiting for transfers between devices: 83.8 us -> none  [partner(): lax.ppermute(value, axis, [(i, i ^ 1 << distance) for i in range(lax.axis...]
    ppermute x6 -> x0, starting transfers between devices: 37.1 us -> none  [partner(): lax.ppermute(value, axis, [(i, i ^ 1 << distance) for i in range(lax.axis...]
    all_to_all x2 -> x0, blocking collectives: 36.3 us -> none  [the longest x1 32.7 us: on_device(): lax.all_to_all(partial_out.astype(jnp.bfloat16), GX, split_axis=0, concat...]
    all_to_all x2 -> x0, starting transfers between devices: 25.1 us -> none  [the longest x1 16.3 us: turned_blocks(): out = lax.all_to_all(out, axes[k], k, k, tiled=True)]
    all_to_all x2 -> x0, waiting for transfers between devices: 21.6 us -> none  [the longest x1 11.2 us: turned_blocks(): out = lax.all_to_all(out, axes[k], k, k, tiled=True)]
    unnamed x26 -> x1, local copies, waits for them, and re-layouts: 17.5 us -> 1.41 us
  transfers between devices with their start and end apart: 10 -> 0, of which waited for: 10 -> 0; matrix products, arithmetic and copies ran while one was open for 5% -> 0% of each run, Pallas kernels for 0% -> 0%
where the time goes in v1:
time: 120 us
  Pallas kernels  118 us (98%)
  local copies, waits for them, and re-layouts  1.41 us (1%)
    pallas_call x1, Pallas kernels, on_device(): pl.pallas_call(functools.partial(layer_kernel, cfg), out_shape=jax.ShapeD...  118 us

profile of v1, /device:TPU:33, one launch (start us, length us, event | category | flops | bytes accessed | tf_op | source)
XLA Modules:
  0.0 120.2 jit_solution(4662049688075289869)
XLA Ops:
  0.7 118.1 %layer.1 = bf16[1,8192]{1,0:T(2,128)(2,1)} custom-call(s32[1]{0:T(128)S(6)} %copy.16.lengths, s32[1,2]{1,0:T(1,128)} %route_ids.1, f32[1,2]{1,0:T(1,128)} %route_scores.1, bf16[1,8192]{1,0:T(2,128)(2,1)} %stream_in.1, bf16[1,8192]{1,0:T(2,128)(2,1)} %query.1, bf16[1,1024]{1,0:T(2,128)(2,1)} %key_new.1, bf16[1,1024]{1,0:T(2,128)(2,1)} %value_new.1, ...), custom_call_target="tpu_custom_call" | custom-call | tf_op jit(solution)/shard_map/layer/pallas_call | solution.py:595
  118.8 1.4 %copy.17 = bf16[1,8192]{1,0:T(2,128)(2,1)} copy(bf16[1,8192]{1,0:T(2,128)(2,1)} %layer.1) | data formatting | bytes 32768

commit v2 on v1

--- a/solution.py
+++ b/solution.py
@@ -101,9 +101,17 @@
     lf,
     lout,
     lbuf,
+    svm,
+    qvm,
+    knvm,
+    vnvm,
+    gainvm,
     loc_sem,
     one_send,
     one_recv,
+    z_recv,
+    tok,
+    size_send,
     st_send,
     st_recv,
     me_send,
@@ -120,10 +128,12 @@
     width = cfg["width"]
     bw = width // MSPLIT
     pieces = cfg["hidden"] // LANES
-    per = cfg["per"]
+    edges = cfg["edges"]
     pad = cfg["pad"]
+    short = cfg["short"]
     quarters = MSPLIT // RESIDENT
     rows = quarters * pad
+    hops = MSPLIT - 1
 
     me = lax.axis_index("gx")
     z = me // PLANE
@@ -133,15 +143,20 @@
     low = me - m * hsplit
     sgn = 1 - 2 * lax.rem(me, 2)
 
-    barrier = pltpu.get_barrier_semaphore()
-
-    def greet(i):
-        pl.semaphore_signal(
-            barrier, inc=1, device_id={"gx": lax.rem(me + i, n)}, device_id_type=MESH
+    def up(step):
+        return lax.rem(z + sgn * step + 2 * planes, planes)
+
+    def signal(sem, target):
+        pl.semaphore_signal(sem, inc=1, device_id={"gx": target}, device_id_type=MESH)
+
+    small = [
+        pltpu.make_async_copy(src, dst, loc_sem.at[6 + i])
+        for i, (src, dst) in enumerate(
+            [(query, qvm), (key_new, knvm), (value_new, vnvm), (stream_in, svm), (gain, gainvm)]
         )
-
-    each(n, greet, 1)
-
+    ]
+    for load in small:
+        load.start()
     loads = [
         pltpu.make_async_copy(key_cache, kbuf, loc_sem.at[0]),
         pltpu.make_async_copy(value_cache, vbuf, loc_sem.at[1]),
@@ -152,14 +167,21 @@
             out_weight.at[:, pl.ds(pl.multiple_of(k * bw, bw), bw)], wbuf.at[k], loc_sem.at[5]
         ),
     ]
-    for load in loads:
+    for load in loads[:2]:
         load.start()
 
-    for j in range(width // LANES):
-        cols = slice(j * LANES, (j + 1) * LANES)
-        qf[j : j + 1, :] = query[0:1, cols].astype(F32)
-        sf[j : j + 1, :] = stream_in[0:1, cols].astype(F32)
-    sblk[...] = sf[...].reshape(MSPLIT, 8, LANES).astype(BF16)
+    barrier = pltpu.get_barrier_semaphore()
+
+    for step in (1, -1):
+        signal(barrier, up(step) * PLANE + k)
+
+    def greet(i):
+        signal(barrier, z * PLANE + lax.rem(k + i, PLANE))
+
+    each(PLANE, greet, 1)
+
+    for load in loads[2:]:
+        load.start()
 
     lane = lax.broadcasted_iota(jnp.int32, (1, LANES), 1)
     s0 = jnp.full((1, LANES), route_scores[0, 0], F32)
@@ -180,28 +202,50 @@
         meta = jnp.where(lane == RESIDENT + e, picked, meta)
     meta_out[...] = meta
 
+    for load in small[:3]:
+        load.wait()
+    for j in range(width // LANES):
+        qf[j : j + 1, :] = qvm[0:1, j * LANES : (j + 1) * LANES].astype(F32)
+
+    def per_group(row_ref):
+        return jnp.concatenate(
+            [
+                jnp.broadcast_to(row_ref[0:1, g * HS : (g + 1) * HS].astype(F32), (NH // KVH, HS))
+                for g in range(KVH)
+            ],
+            axis=0,
+        )
+
+    q_all = qf[...]
+    scale = HS ** (-0.5)
+    o = jnp.sum(q_all * per_group(knvm), axis=1, keepdims=True) * scale
+    v_own = per_group(vnvm)
     loads[0].wait()
+    slots = kbuf.shape[0]
+    s = jnp.concatenate(
+        [
+            nt_dot(q_all[g * 8 : (g + 1) * 8].astype(BF16), kbuf[:, g * HS : (g + 1) * HS])
+            for g in range(KVH)
+        ],
+        axis=0,
+    )
+    live = lax.broadcasted_iota(jnp.int32, (NH, slots), 1) < lengths[0]
+    s = jnp.where(live, s * scale, -1e30)
+    t = jnp.maximum(jnp.max(s, axis=1, keepdims=True), o)
+    es = jnp.exp(s - t)
+    eo = jnp.exp(o - t)
+    total = jnp.sum(es, axis=1, keepdims=True) + eo
+    p = es / total
+    own_term = (eo / total).astype(BF16).astype(F32) * v_own
     loads[1].wait()
-    scale = HS ** (-0.5)
-    slots = kbuf.shape[0]
-    live = lax.broadcasted_iota(jnp.int32, (NH // KVH, slots), 1) < lengths[0]
     for g in range(KVH):
-        cols = slice(g * HS, (g + 1) * HS)
-        q_g = qf[g * 8 : (g + 1) * 8, :]
-        k_own = key_new[0:1, cols].astype(F32)
-        v_own = value_new[0:1, cols].astype(F32)
-        s = nt_dot(q_g.astype(BF16), kbuf[:, cols]) * scale
-        s = jnp.where(live, s, -1e30)
-        o = jnp.sum(q_g * k_own, axis=1, keepdims=True) * scale
-        t = jnp.maximum(jnp.max(s, axis=1, keepdims=True), o)
-        es = jnp.exp(s - t)
-        eo = jnp.exp(o - t)
-        total = jnp.sum(es, axis=1, keepdims=True) + eo
-        p = (es / total).astype(BF16)
-        po = (eo / total).astype(BF16).astype(F32)
-        att[g] = (nn_dot(p, vbuf[:, cols]) + po * v_own).astype(BF16)
-
-    pl.semaphore_wait(barrier, n - 1)
+        r = slice(g * 8, (g + 1) * 8)
+        mixed = nn_dot(p[r].astype(BF16), vbuf[:, g * HS : (g + 1) * HS])
+        att[g] = (mixed + own_term[r]).astype(BF16)
+
+    pl.semaphore_wait(barrier, PLANE + 1)
+    for step in (1, -1):
+        signal(tok.at[0], up(step) * PLANE + k)
 
     def plane_send(i):
         j = lax.rem(k + i, PLANE)
@@ -223,6 +267,46 @@
 
     each(PLANE, w_send, 1)
 
+    abuf[z, k] = att[k]
+    pl.semaphore_wait(tok.at[0], 2)
+    for step in (2, -2):
+        signal(tok.at[1], up(step) * PLANE + k)
+    wait_bytes(abuf.at[0, pl.ds(0, PLANE - 1)], one_recv.at[0])
+    pl.semaphore_wait(tok.at[1], 2)
+
+    def z_copy(origin, step):
+        return copy_to(
+            abuf.at[origin],
+            abuf.at[origin],
+            one_send.at[2],
+            z_recv.at[origin],
+            up(step) * PLANE + k,
+        )
+
+    reach = planes // 4
+    for step in range(reach, 0, -1):
+        z_copy(z, step).start()
+        z_copy(z, -step).start()
+    for step in (reach, -reach):
+        signal(tok.at[2], up(step) * PLANE + k)
+    for load in small[3:]:
+        load.wait()
+    for j in range(width // LANES):
+        sf[j : j + 1, :] = svm[0:1, j * LANES : (j + 1) * LANES].astype(F32)
+    sblk[...] = sf[...].reshape(MSPLIT, 8, LANES).astype(BF16)
+    far = up(-reach)
+    wait_bytes(abuf.at[far], z_recv.at[far])
+    for step in range(reach, 0, -1):
+        z_copy(far, step).start()
+    near = up(reach)
+    wait_bytes(abuf.at[near], z_recv.at[near])
+    for step in range(reach - 1, 0, -1):
+        z_copy(near, -step).start()
+    pl.semaphore_wait(tok.at[2], 2)
+    for step in (1, -1):
+        signal(tok.at[3], up(step) * PLANE + k)
+    pl.semaphore_wait(tok.at[3], 2)
+
     def stream_send(j):
         target = j * hsplit + z
 
@@ -238,30 +322,17 @@
         sbuf[k] = sblk[m]
         meta_in[k] = meta_out[...]
 
-    abuf[z, k] = att[k]
-    wait_bytes(abuf.at[0, pl.ds(0, PLANE - 1)], one_recv.at[0])
-
-    def z_send(i):
-        target = lax.rem(z + i, planes)
-        copy_to(
-            abuf.at[z], abuf.at[z], one_send.at[2], one_recv.at[2], target * PLANE + k
-        ).start()
-
-    each(planes, z_send, 1)
-
-    def stream_recv(i):
-        source = h * PLANE + i
-
-        @pl.when(source != me)
+    def z_wait(i):
+        origin = lax.rem(z + i, planes)
+
+        @pl.when((origin != far) & (origin != near))
         def _():
-            wait_bytes(sbuf.at[i], st_recv.at[i])
-            wait_bytes(meta_in.at[i], me_recv.at[i])
-
-    each(PLANE, stream_recv)
+            wait_bytes(abuf.at[origin], z_recv.at[origin])
+
+    each(planes, z_wait, 1)
 
     loads[5].wait()
     wait_bytes(wbuf.at[pl.ds(0, PLANE - 1)], one_recv.at[1])
-    wait_bytes(abuf.at[pl.ds(0, planes - 1)], one_recv.at[2])
 
     af[...] = abuf[...].reshape(batch * 8, LANES).astype(F32)
     a = jnp.concatenate(
@@ -277,9 +348,19 @@
     each(hsplit, proj_send, 1)
     dbuf[h] = pbuf[h]
 
+    def stream_recv(i):
+        source = h * PLANE + i
+
+        @pl.when(source != me)
+        def _():
+            wait_bytes(sbuf.at[i], st_recv.at[i])
+            wait_bytes(meta_in.at[i], me_recv.at[i])
+
+    each(PLANE, stream_recv)
+
     lf[...] = sbuf[...].reshape(PLANE * 8, LANES).astype(F32)
     stream = jnp.concatenate([lf[pl.ds(c, 8, stride=8), :] for c in range(8)], axis=1)
-    g8 = gain[pl.ds(pl.multiple_of(m * 8, 8), 8), :]
+    g8 = gainvm[pl.ds(pl.multiple_of(m * 8, 8), 8), :]
     gain_row = jnp.concatenate([g8[c : c + 1, :] for c in range(8)], axis=1)
     route = jnp.concatenate([meta_in[i] for i in range(PLANE)], axis=0)
 
@@ -320,7 +401,9 @@
     def place_of(rank, picked):
         out = rank
         for c in range(1, quarters):
-            out = out + jnp.where(rank >= float(c * per), float(pad - per), 0.0)
+            step = float(c * pad - edges[c] - (c - 1) * pad + edges[c - 1])
+            if step:
+                out = out + jnp.where(rank >= float(edges[c]), step, 0.0)
         return jnp.where(picked > 0.5, out, -1.0)
 
     rows_i = [place_of(ranks_t[RESIDENT + e : RESIDENT + e + 1], info_t[RESIDENT + e : RESIDENT + e + 1]) for e in range(RESIDENT)]
@@ -352,10 +435,31 @@
     next_dev = ring(1) * hsplit + low
     prev_dev = ring(-1) * hsplit + low
 
-    def rs_copy(slot, q, target):
-        return copy_to(
-            rs_send.at[slot, q], rs_recv.at[slot, q], one_send.at[7], rs_sem.at[slot, q], target
-        )
+    def sized(chunk, body):
+        odd = lax.rem(chunk, 2)
+
+        @pl.when(odd == 0)
+        def _():
+            body(pl.ds(0, pad), 0)
+
+        @pl.when(odd == 1)
+        def _():
+            body(pl.ds(0, short), 1)
+
+    def rs_start(slot, q, chunk, target):
+        def go(r, kind):
+            copy_to(
+                rs_send.at[slot, q, r],
+                rs_recv.at[slot, q, r],
+                size_send.at[kind],
+                rs_sem.at[slot, q],
+                target,
+            ).start()
+
+        sized(chunk, go)
+
+    def rs_wait(slot, q, chunk):
+        sized(chunk, lambda r, kind: wait_bytes(rs_recv.at[slot, q, r], rs_sem.at[slot, q]))
 
     def first(q):
         cols = pl.ds(pl.multiple_of(q * LANES, LANES), LANES)
@@ -364,25 +468,27 @@
             r = nn_dot(xcs[e], rhs)
             own[q, e * quarters : (e + 1) * quarters] = r.reshape(quarters, pad, 2 * LANES)
         rs_send[0, q] = own[q, ring(fwd)].astype(BF16)
-        rs_copy(0, q, next_dev).start()
+        rs_start(0, q, ring(fwd), next_dev)
         rs_send[fwd, q] = own[q, ring(-bwd)].astype(BF16)
-        rs_copy(fwd, q, prev_dev).start()
+        rs_start(fwd, q, ring(-bwd), prev_dev)
 
     each(pieces, first)
 
     for t in range(1, fwd):
 
         def onward(q, t=t):
-            wait_bytes(rs_recv.at[t - 1, q], rs_sem.at[t - 1, q])
-            v = rs_recv[t - 1, q].astype(F32) + own[q, ring(fwd - t)]
+            chunk = ring(fwd - t)
+            rs_wait(t - 1, q, chunk)
+            v = rs_recv[t - 1, q].astype(F32) + own[q, chunk]
             rs_send[t, q] = v.astype(BF16)
-            rs_copy(t, q, next_dev).start()
+            rs_start(t, q, chunk, next_dev)
             if t < bwd:
                 b = fwd + t
-                wait_bytes(rs_recv.at[b - 1, q], rs_sem.at[b - 1, q])
-                v = rs_recv[b - 1, q].astype(F32) + own[q, ring(t - bwd)]
+                chunk = ring(t - bwd)
+                rs_wait(b - 1, q, chunk)
+                v = rs_recv[b - 1, q].astype(F32) + own[q, chunk]
                 rs_send[b, q] = v.astype(BF16)
-                rs_copy(b, q, prev_dev).start()
+                rs_start(b, q, chunk, prev_dev)
 
         each(pieces, onward)
 
@@ -396,48 +502,67 @@
     mean = jnp.sum(jnp.where(hit, power, 0.0), axis=1, keepdims=True) / float(width)
     factor = lax.rsqrt(mean + 1e-05)
 
-    def ag_copy(slot, q, chunk, target):
-        return copy_to(
-            hbuf.at[q, chunk], hbuf.at[q, chunk], one_send.at[8], ag_sem.at[slot, q], target
-        )
+    def ag_start(slot, q, chunk, target):
+        def go(r, kind):
+            copy_to(
+                hbuf.at[q, chunk, r],
+                hbuf.at[q, chunk, r],
+                size_send.at[2 + kind],
+                ag_sem.at[slot, q],
+                target,
+            ).start()
+
+        sized(chunk, go)
+
+    def ag_wait(slot, q, chunk):
+        sized(chunk, lambda r, kind: wait_bytes(hbuf.at[q, chunk, r], ag_sem.at[slot, q]))
 
     def finish(q):
-        wait_bytes(rs_recv.at[fwd - 1, q], rs_sem.at[fwd - 1, q])
-        wait_bytes(rs_recv.at[MSPLIT - 2, q], rs_sem.at[MSPLIT - 2, q])
+        rs_wait(fwd - 1, q, m)
+        rs_wait(MSPLIT - 2, q, m)
         v = own[q, m] + rs_recv[fwd - 1, q].astype(F32) + rs_recv[MSPLIT - 2, q].astype(F32)
         v = v * factor
         ga = v[:, :LANES]
-        up = v[:, LANES:]
-        hbuf[q, m] = (ga / (1.0 + jnp.exp(-ga)) * up).astype(BF16)
-        ag_copy(0, q, m, next_dev).start()
-        ag_copy(fwd, q, m, prev_dev).start()
+        up_half = v[:, LANES:]
+        hbuf[q, m] = (ga / (1.0 + jnp.exp(-ga)) * up_half).astype(BF16)
+        ag_start(0, q, m, next_dev)
+        ag_start(fwd, q, m, prev_dev)
 
     each(pieces, finish)
 
     for t in range(1, fwd):
 
         def relay(q, t=t):
-            wait_bytes(hbuf.at[q, ring(-t)], ag_sem.at[t - 1, q])
-            ag_copy(t, q, ring(-t), next_dev).start()
+            ag_wait(t - 1, q, ring(-t))
+            ag_start(t, q, ring(-t), next_dev)
             if t < bwd:
                 b = fwd + t
-                wait_bytes(hbuf.at[q, ring(t)], ag_sem.at[b - 1, q])
-                ag_copy(b, q, ring(t), prev_dev).start()
+                ag_wait(b - 1, q, ring(t))
+                ag_start(b, q, ring(t), prev_dev)
 
         each(pieces, relay)
 
     def arrived(q):
-        wait_bytes(hbuf.at[q, ring(-fwd)], ag_sem.at[fwd - 1, q])
-        wait_bytes(hbuf.at[q, ring(bwd)], ag_sem.at[MSPLIT - 2, q])
+        ag_wait(fwd - 1, q, ring(-fwd))
+        ag_wait(MSPLIT - 2, q, ring(bwd))
 
     each(pieces, arrived)
 
     loads[4].wait()
     col_iota = lax.broadcasted_iota(jnp.int32, (batch, rows), 1).astype(F32)
+    row_iota = lax.broadcasted_iota(jnp.int32, (rows, LANES), 0)
+    filled = lax.rem(row_iota, 2 * pad) < pad + short
     spreads = []
     for e in range(RESIDENT):
         hc = jnp.concatenate(
-            [hbuf[q, e * quarters : (e + 1) * quarters].reshape(rows, LANES) for q in range(pieces)],
+            [
+                jnp.where(
+                    filled,
+                    hbuf[q, e * quarters : (e + 1) * quarters].astype(F32).reshape(rows, LANES),
+                    0.0,
+                ).astype(BF16)
+                for q in range(pieces)
+            ],
             axis=1,
         )
         pick = jnp.where(col_iota == cols_i[e], 1.0, 0.0).astype(BF16)
@@ -485,8 +610,18 @@
     wait_bytes(meta_all.at[pl.ds(0, hsplit - 1)], one_send.at[4])
     wait_bytes(xbuf.at[pl.ds(0, hsplit - 1)], one_send.at[5])
     wait_bytes(ssq_all.at[pl.ds(0, MSPLIT - 1)], one_send.at[6])
-    wait_bytes(rs_send, one_send.at[7])
-    wait_bytes(hbuf.at[:, pl.ds(0, MSPLIT - 1)], one_send.at[8])
+    for parity in range(2):
+
+        @pl.when(lax.rem(m, 2) == parity)
+        def _(parity=parity):
+            rs_even = MSPLIT // 2 - (1 - parity)
+            ag_steps = list(range(fwd)) + list(range(bwd))
+            ag_even = sum((parity + step) % 2 == 0 for step in ag_steps)
+            wait_bytes(rs_send.at[pl.ds(0, rs_even)], size_send.at[0])
+            wait_bytes(rs_send.at[pl.ds(0, hops - rs_even), :, pl.ds(0, short)], size_send.at[1])
+            wait_bytes(hbuf.at[:, pl.ds(0, ag_even)], size_send.at[2])
+            wait_bytes(hbuf.at[:, pl.ds(0, hops - ag_even), pl.ds(0, short)], size_send.at[3])
+
     wait_bytes(kin.at[pl.ds(0, hsplit - 1)], one_send.at[9])
 
     def drain(j):
@@ -504,7 +639,7 @@
 
     qf[...] = lbuf[...].reshape(MSPLIT * 8, LANES).astype(F32)
     for j in range(width // LANES):
-        out_ref[0:1, j * LANES : (j + 1) * LANES] = qf[j : j + 1, :].astype(BF16)
+        out_ref[0:1, j * LANES : (j + 1) * LANES] = qf[j : j + 1, :]
 
 
 def on_device(
@@ -533,10 +668,13 @@
     planes = n // PLANE
     cols = out_weight.shape[1]
     quarters = MSPLIT // RESIDENT
-    per = -(-(5 * n // 8) // quarters)
-    pad = -(-per // 8) * 8
+    cap = 5 * n // 8
+    edges = [-(-(cap * c // quarters) // 8) * 8 for c in range(quarters + 1)]
+    pad = edges[1] - edges[0]
+    short = edges[2] - edges[1]
+    assert [b - a for a, b in zip(edges, edges[1:])] == [pad, short] * (quarters // 2)
     pieces = hidden // LANES
-    cfg = dict(n=n, width=width, hidden=hidden, per=per, pad=pad)
+    cfg = dict(n=n, width=width, hidden=hidden, edges=edges, pad=pad, short=short)
     hops = MSPLIT - 1
 
     def vmem(*shape, dtype=BF16):
@@ -577,9 +715,17 @@
         vmem(PLANE * 8, LANES, dtype=F32),
         vmem(PLANE, 8, LANES),
         vmem(MSPLIT, 8, LANES),
-        pltpu.SemaphoreType.DMA((6,)),
+        vmem(1, width),
+        vmem(1, width),
+        vmem(1, kv),
+        vmem(1, kv),
+        vmem(width // LANES, LANES, dtype=F32),
+        pltpu.SemaphoreType.DMA((11,)),
         pltpu.SemaphoreType.DMA((10,)),
         pltpu.SemaphoreType.DMA((8,)),
+        pltpu.SemaphoreType.DMA((planes,)),
+        pltpu.SemaphoreType.REGULAR((4,)),
+        pltpu.SemaphoreType.DMA((4,)),
         pltpu.SemaphoreType.DMA((MSPLIT,)),
         pltpu.SemaphoreType.DMA((PLANE,)),
         pltpu.SemaphoreType.DMA((MSPLIT,)),
@@ -594,8 +740,8 @@
     anywhere = pl.BlockSpec(memory_space=pl.ANY)
     return pl.pallas_call(
         functools.partial(layer_kernel, cfg),
-        out_shape=jax.ShapeDtypeStruct((1, width), BF16),
-        in_specs=[smem] * 3 + [local] * 5 + [anywhere] * 6,
+        out_shape=jax.ShapeDtypeStruct((1, width), F32),
+        in_specs=[smem] * 3 + [anywhere] * 11,
         out_specs=local,
         scratch_shapes=scratch,
         compiler_params=pltpu.CompilerParams(
@@ -617,7 +763,7 @@
         gate_weight,
         up_weight,
         down_weight,
-    )
+    ).astype(BF16)
 
 
 def solution(mesh):

time: 120 us -> 104 us (0.87)
  Pallas kernels: 118 us -> 102 us
  local copies, waits for them, and re-layouts: 1.41 us -> 0 us
  other arithmetic: 0 us -> 1.4 us
    pallas_call x1, Pallas kernels: 118 us -> 102 us  [on_device(): pl.pallas_call(functools.partial(layer_kernel, cfg), out_shape=jax.ShapeD...]
    unnamed x1 -> x0, local copies, waits for them, and re-layouts: 1.41 us -> none
    convert_element_type x0 -> x1, other arithmetic: none -> 1.4 us  [on_device(): return pl.pallas_call(functools.partial(layer_kernel, cfg), out_shape=jax...]
where the time goes in v2:
time: 104 us
  Pallas kernels  102 us (98%)
  other arithmetic  1.4 us (1%)
    pallas_call x1, Pallas kernels, on_device(): pl.pallas_call(functools.partial(layer_kernel, cfg), out_shape=jax.ShapeD...  102 us

profile of v2, /device:TPU:33, one launch (start us, length us, event | category | flops | bytes accessed | tf_op | source)
XLA Modules:
  0.0 104.2 jit_solution(1798494203306716567)
XLA Ops:
  0.7 102.2 %layer.1 = f32[1,8192]{1,0:T(1,128)} custom-call(s32[1]{0:T(128)S(6)} %copy.15.lengths, s32[1,2]{1,0:T(1,128)} %route_ids.1, f32[1,2]{1,0:T(1,128)} %route_scores.1, bf16[1,8192]{1,0:T(2,128)(2,1)} %stream_in.1, bf16[1,8192]{1,0:T(2,128)(2,1)} %query.1, bf16[1,1024]{1,0:T(2,128)(2,1)} %key_new.1, bf16[1,1024]{1,0:T(2,128)(2,1)} %value_new.1, ...), custom_call_target="tpu_custom_call" | custom-call | tf_op jit(solution)/shard_map/layer/pallas_call | solution.py:741
  102.8 1.4 %convert_element_type.3 = bf16[1,8192]{1,0:T(2,128)(2,1)} convert(f32[1,8192]{1,0:T(1,128)} %layer.1) | non-fusion elementwise | flops 8192 | bytes 49152 | tf_op jit(solution)/shard_map/convert_element_type | solution.py:766

commit v3 on v2

--- a/solution.py
+++ b/solution.py
@@ -52,9 +52,9 @@
 
 def layer_kernel(
     cfg,
-    lengths,
-    route_ids,
-    route_scores,
+    lengths_in,
+    ids_in,
+    scores_in,
     stream_in,
     query,
     key_new,
@@ -106,6 +106,15 @@
     knvm,
     vnvm,
     gainvm,
+    lengths,
+    route_ids,
+    route_scores,
+    pst,
+    pme,
+    route_blk,
+    route_all,
+    acc,
+    picks,
     loc_sem,
     one_send,
     one_recv,
@@ -152,7 +161,16 @@
     small = [
         pltpu.make_async_copy(src, dst, loc_sem.at[6 + i])
         for i, (src, dst) in enumerate(
-            [(query, qvm), (key_new, knvm), (value_new, vnvm), (stream_in, svm), (gain, gainvm)]
+            [
+                (query, qvm),
+                (key_new, knvm),
+                (value_new, vnvm),
+                (lengths_in, lengths),
+                (stream_in, svm),
+                (gain, gainvm),
+                (ids_in, route_ids),
+                (scores_in, route_scores),
+            ]
         )
     ]
     for load in small:
@@ -170,6 +188,20 @@
     for load in loads[:2]:
         load.start()
 
+    xs = k // 2
+    core = lax.rem(k, 2)
+
+    def peer(dx, dc):
+        return 2 * lax.rem(xs + dx, PLANE // 2) + lax.rem(core + dc, 2)
+
+    plane_steps = [(dx, dc) for dx in (2, 3, 1) for dc in (0, 1)] + [(0, 1)]
+    patch_steps = [(dz, dx, dc) for dx in (2, 3, 1) for dz in (1, 0) for dc in (0, 1)]
+    patch_steps += [(1, 0, 0), (1, 0, 1), (0, 0, 1)]
+
+    def patch_peer(step):
+        dz, dx, dc = step
+        return lax.rem(h // PLANE + dz, 2) * PLANE + peer(dx, dc)
+
     barrier = pltpu.get_barrier_semaphore()
 
     for step in (1, -1):
@@ -183,26 +215,7 @@
     for load in loads[2:]:
         load.start()
 
-    lane = lax.broadcasted_iota(jnp.int32, (1, LANES), 1)
-    s0 = jnp.full((1, LANES), route_scores[0, 0], F32)
-    s1 = jnp.full((1, LANES), route_scores[0, 1], F32)
-    top = jnp.maximum(s0, s1)
-    e0 = jnp.exp(s0 - top)
-    e1 = jnp.exp(s1 - top)
-    q0 = e0 / (e0 + e1)
-    q1 = e1 / (e0 + e1)
-    id0 = jnp.full((1, LANES), route_ids[0, 0], jnp.int32)
-    id1 = jnp.full((1, LANES), route_ids[0, 1], jnp.int32)
-    meta = jnp.zeros((1, LANES), F32)
-    for e in range(RESIDENT):
-        w = jnp.where(id0 == e, q0, 0.0) + jnp.where(id1 == e, q1, 0.0)
-        w = w.astype(BF16).astype(F32)
-        picked = jnp.where((id0 == e) | (id1 == e), 1.0, 0.0)
-        meta = jnp.where(lane == e, w, meta)
-        meta = jnp.where(lane == RESIDENT + e, picked, meta)
-    meta_out[...] = meta
-
-    for load in small[:3]:
+    for load in small[:4]:
         load.wait()
     for j in range(width // LANES):
         qf[j : j + 1, :] = qvm[0:1, j * LANES : (j + 1) * LANES].astype(F32)
@@ -247,16 +260,61 @@
     for step in (1, -1):
         signal(tok.at[0], up(step) * PLANE + k)
 
-    def plane_send(i):
-        j = lax.rem(k + i, PLANE)
+    for step in plane_steps:
+        j = peer(*step)
         copy_to(
             att.at[j], abuf.at[z, k], one_send.at[0], one_recv.at[0], z * PLANE + j
         ).start()
 
-    each(PLANE, plane_send, 1)
-
-    def w_send(i):
-        j = lax.rem(k + i, PLANE)
+    abuf[z, k] = att[k]
+    for step in plane_steps:
+        signal(tok.at[3], z * PLANE + peer(*step))
+
+    pl.semaphore_wait(tok.at[0], 2)
+    for step in (2, -2):
+        signal(tok.at[1], up(step) * PLANE + k)
+
+    for load in small[4:]:
+        load.wait()
+    for j in range(width // LANES):
+        sf[j : j + 1, :] = svm[0:1, j * LANES : (j + 1) * LANES].astype(F32)
+    sblk[...] = sf[...].reshape(MSPLIT, 8, LANES).astype(BF16)
+    lane = lax.broadcasted_iota(jnp.int32, (1, LANES), 1)
+    s0 = jnp.full((1, LANES), route_scores[0, 0], F32)
+    s1 = jnp.full((1, LANES), route_scores[0, 1], F32)
+    top = jnp.maximum(s0, s1)
+    e0 = jnp.exp(s0 - top)
+    e1 = jnp.exp(s1 - top)
+    q0 = e0 / (e0 + e1)
+    q1 = e1 / (e0 + e1)
+    id0 = jnp.full((1, LANES), route_ids[0, 0], jnp.int32)
+    id1 = jnp.full((1, LANES), route_ids[0, 1], jnp.int32)
+    meta = jnp.zeros((1, LANES), F32)
+    for e in range(RESIDENT):
+        w = jnp.where(id0 == e, q0, 0.0) + jnp.where(id1 == e, q1, 0.0)
+        w = w.astype(BF16).astype(F32)
+        picked = jnp.where((id0 == e) | (id1 == e), 1.0, 0.0)
+        meta = jnp.where(lane == e, w, meta)
+        meta = jnp.where(lane == RESIDENT + e, picked, meta)
+    meta_out[...] = meta
+
+    gatherer = lax.rem(z, PLANE)
+
+    @pl.when(k != gatherer)
+    def _():
+        target = z * PLANE + gatherer
+        copy_to(sblk, pst.at[:, k], st_send.at[0], st_recv.at[0], target).start()
+        copy_to(meta_out, pme.at[k], me_send.at[0], me_recv.at[0], target).start()
+
+    @pl.when(k == gatherer)
+    def _():
+        for j in range(MSPLIT):
+            pst[j, k] = sblk[j]
+        pme[k] = meta_out[...]
+
+    pl.semaphore_wait(tok.at[3], PLANE - 1)
+    for step in plane_steps:
+        j = peer(*step)
         copy_to(
             out_weight.at[:, pl.ds(pl.multiple_of(j * bw, bw), bw)],
             wbuf.at[k],
@@ -265,12 +323,6 @@
             z * PLANE + j,
         ).start()
 
-    each(PLANE, w_send, 1)
-
-    abuf[z, k] = att[k]
-    pl.semaphore_wait(tok.at[0], 2)
-    for step in (2, -2):
-        signal(tok.at[1], up(step) * PLANE + k)
     wait_bytes(abuf.at[0, pl.ds(0, PLANE - 1)], one_recv.at[0])
     pl.semaphore_wait(tok.at[1], 2)
 
@@ -289,11 +341,27 @@
         z_copy(z, -step).start()
     for step in (reach, -reach):
         signal(tok.at[2], up(step) * PLANE + k)
-    for load in small[3:]:
-        load.wait()
-    for j in range(width // LANES):
-        sf[j : j + 1, :] = svm[0:1, j * LANES : (j + 1) * LANES].astype(F32)
-    sblk[...] = sf[...].reshape(MSPLIT, 8, LANES).astype(BF16)
+    @pl.when(k == gatherer)
+    def _():
+        pl.semaphore_wait(tok.at[2], 2)
+        wait_bytes(pst.at[pl.ds(0, PLANE - 1)], st_recv.at[0])
+        wait_bytes(pme.at[pl.ds(0, PLANE - 1)], me_recv.at[0])
+
+        def hand_on(j):
+            target = j * hsplit + z
+
+            @pl.when(target != me)
+            def _():
+                copy_to(pst.at[j], sbuf, st_send.at[1], st_recv.at[1], target).start()
+                copy_to(pme, meta_in, me_send.at[1], me_recv.at[1], target).start()
+
+            @pl.when(target == me)
+            def _():
+                sbuf[...] = pst[j]
+                meta_in[...] = pme[...]
+
+        each(MSPLIT, hand_on)
+
     far = up(-reach)
     wait_bytes(abuf.at[far], z_recv.at[far])
     for step in range(reach, 0, -1):
@@ -302,25 +370,9 @@
     wait_bytes(abuf.at[near], z_recv.at[near])
     for step in range(reach - 1, 0, -1):
         z_copy(near, -step).start()
-    pl.semaphore_wait(tok.at[2], 2)
-    for step in (1, -1):
-        signal(tok.at[3], up(step) * PLANE + k)
-    pl.semaphore_wait(tok.at[3], 2)
-
-    def stream_send(j):
-        target = j * hsplit + z
-
-        @pl.when(target != me)
-        def _():
-            copy_to(sblk.at[j], sbuf.at[k], st_send.at[j], st_recv.at[k], target).start()
-            copy_to(meta_out, meta_in.at[k], me_send.at[j], me_recv.at[k], target).start()
-
-    each(MSPLIT, stream_send)
-
-    @pl.when(z == h)
+    @pl.when(k != gatherer)
     def _():
-        sbuf[k] = sblk[m]
-        meta_in[k] = meta_out[...]
+        pl.semaphore_wait(tok.at[2], 2)
 
     def z_wait(i):
         origin = lax.rem(z + i, planes)
@@ -341,55 +393,50 @@
     part = nt_dot(a, wbuf[...].reshape(PLANE * wbuf.shape[1], bw))
     pbuf[...] = part.astype(BF16).reshape(hsplit, 8, part.shape[1])
 
-    def proj_send(i):
-        j = lax.rem(h + i, hsplit)
+    for step in patch_steps:
+        j = patch_peer(step)
         copy_to(pbuf.at[j], dbuf.at[h], one_send.at[3], one_recv.at[3], m * hsplit + j).start()
-
-    each(hsplit, proj_send, 1)
     dbuf[h] = pbuf[h]
 
-    def stream_recv(i):
-        source = h * PLANE + i
-
-        @pl.when(source != me)
-        def _():
-            wait_bytes(sbuf.at[i], st_recv.at[i])
-            wait_bytes(meta_in.at[i], me_recv.at[i])
-
-    each(PLANE, stream_recv)
-
+    @pl.when(z != h)
+    def _():
+        wait_bytes(sbuf, st_recv.at[1])
+        wait_bytes(meta_in, me_recv.at[1])
+
+    route_blk[...] = jnp.concatenate([meta_in[i] for i in range(PLANE)], axis=0)
+    route_all[h] = route_blk[...]
+    for step in patch_steps:
+        target = m * hsplit + patch_peer(step)
+        copy_to(route_blk, route_all.at[h], one_send.at[10], one_recv.at[8], target).start()
     lf[...] = sbuf[...].reshape(PLANE * 8, LANES).astype(F32)
     stream = jnp.concatenate([lf[pl.ds(c, 8, stride=8), :] for c in range(8)], axis=1)
     g8 = gainvm[pl.ds(pl.multiple_of(m * 8, 8), 8), :]
     gain_row = jnp.concatenate([g8[c : c + 1, :] for c in range(8)], axis=1)
-    route = jnp.concatenate([meta_in[i] for i in range(PLANE)], axis=0)
 
     wait_bytes(dbuf.at[pl.ds(0, hsplit - 1)], one_recv.at[3])
     halves = []
     for half in range(hsplit // PLANE):
-        acc = dbuf[half * PLANE].astype(F32)
+        part_sum = dbuf[half * PLANE].astype(F32)
         for j in range(1, PLANE):
-            acc = acc + dbuf[half * PLANE + j].astype(F32)
-        halves.append(acc)
+            part_sum = part_sum + dbuf[half * PLANE + j].astype(F32)
+        halves.append(part_sum)
     proj = jnp.concatenate(halves, axis=1).astype(BF16).astype(F32)
     resid = stream + proj
     resid_ref[...] = resid
-    ssq = jnp.sum(resid * resid, axis=1, keepdims=True)
-    lane8 = lax.broadcasted_iota(jnp.int32, (8, LANES), 1)
-    meta_blk[...] = jnp.where(lane8 == 2 * RESIDENT, ssq, route)
-    meta_all[h] = meta_blk[...]
     yblk[...] = (resid * gain_row).astype(BF16)
     xbuf[h] = yblk[...]
-
-    def spread(i):
-        target = m * hsplit + lax.rem(h + i, hsplit)
+    for step in patch_steps:
+        target = m * hsplit + patch_peer(step)
+        copy_to(yblk, xbuf.at[h], one_send.at[5], one_recv.at[5], target).start()
+    ssq = jnp.sum(resid * resid, axis=1, keepdims=True)
+    meta_blk[...] = jnp.broadcast_to(ssq, (8, LANES))
+    meta_all[h] = meta_blk[...]
+    for step in patch_steps:
+        target = m * hsplit + patch_peer(step)
         copy_to(meta_blk, meta_all.at[h], one_send.at[4], one_recv.at[4], target).start()
-        copy_to(yblk, xbuf.at[h], one_send.at[5], one_recv.at[5], target).start()
-
-    each(hsplit, spread, 1)
-    wait_bytes(meta_all.at[pl.ds(0, hsplit - 1)], one_recv.at[4])
-
-    info = meta_all[...].reshape(batch, LANES)
+
+    wait_bytes(route_all.at[pl.ds(0, hsplit - 1)], one_recv.at[8])
+    info = route_all[...].reshape(batch, LANES)
     info_t = info.T
     ia = lax.broadcasted_iota(jnp.int32, (batch, batch), 0)
     ib = lax.broadcasted_iota(jnp.int32, (batch, batch), 1)
@@ -408,15 +455,6 @@
 
     rows_i = [place_of(ranks_t[RESIDENT + e : RESIDENT + e + 1], info_t[RESIDENT + e : RESIDENT + e + 1]) for e in range(RESIDENT)]
     cols_i = [place_of(ranks[:, RESIDENT + e : RESIDENT + e + 1], info[:, RESIDENT + e : RESIDENT + e + 1]) for e in range(RESIDENT)]
-    ssq_row[...] = info_t[2 * RESIDENT : 2 * RESIDENT + 1]
-    ssq_all[m] = ssq_row[...]
-
-    def ssq_send(i):
-        j = lax.rem(m + i, MSPLIT)
-        copy_to(ssq_row, ssq_all.at[m], one_send.at[6], one_recv.at[6], j * hsplit + low).start()
-
-    each(MSPLIT, ssq_send, 1)
-
     wait_bytes(xbuf.at[pl.ds(0, hsplit - 1)], one_recv.at[5])
     x = xbuf[...].reshape(batch, bw)
     r_iota = lax.broadcasted_iota(jnp.int32, (rows, batch), 0).astype(F32)
@@ -429,11 +467,12 @@
     fwd = MSPLIT // 2
     bwd = MSPLIT - 1 - fwd
 
-    def ring(step):
-        return lax.rem(m + sgn * step + 2 * MSPLIT, MSPLIT)
-
-    next_dev = ring(1) * hsplit + low
-    prev_dev = ring(-1) * hsplit + low
+    def ring(q, step):
+        turn = sgn * (1 - 2 * (q // fwd))
+        return lax.rem(m + turn * step + 2 * MSPLIT, MSPLIT)
+
+    def ring_dev(q, step):
+        return ring(q, step) * hsplit + low
 
     def sized(chunk, body):
         odd = lax.rem(chunk, 2)
@@ -467,28 +506,38 @@
             rhs = jnp.concatenate([gbuf[e, :, cols], ubuf[e, :, cols]], axis=1)
             r = nn_dot(xcs[e], rhs)
             own[q, e * quarters : (e + 1) * quarters] = r.reshape(quarters, pad, 2 * LANES)
-        rs_send[0, q] = own[q, ring(fwd)].astype(BF16)
-        rs_start(0, q, ring(fwd), next_dev)
-        rs_send[fwd, q] = own[q, ring(-bwd)].astype(BF16)
-        rs_start(fwd, q, ring(-bwd), prev_dev)
+        rs_send[0, q] = own[q, ring(q, fwd)].astype(BF16)
+        rs_start(0, q, ring(q, fwd), ring_dev(q, 1))
+        rs_send[fwd, q] = own[q, ring(q, -bwd)].astype(BF16)
+        rs_start(fwd, q, ring(q, -bwd), ring_dev(q, -1))
 
     each(pieces, first)
 
+    wait_bytes(meta_all.at[pl.ds(0, hsplit - 1)], one_recv.at[4])
+    ssq_row[...] = meta_all[...].reshape(batch, LANES).T[0:1]
+    ssq_all[m] = ssq_row[...]
+
+    def ssq_send(i):
+        j = lax.rem(m + i, MSPLIT)
+        copy_to(ssq_row, ssq_all.at[m], one_send.at[6], one_recv.at[6], j * hsplit + low).start()
+
+    each(MSPLIT, ssq_send, 1)
+
     for t in range(1, fwd):
 
         def onward(q, t=t):
-            chunk = ring(fwd - t)
+            chunk = ring(q, fwd - t)
             rs_wait(t - 1, q, chunk)
             v = rs_recv[t - 1, q].astype(F32) + own[q, chunk]
             rs_send[t, q] = v.astype(BF16)
-            rs_start(t, q, chunk, next_dev)
+            rs_start(t, q, chunk, ring_dev(q, 1))
             if t < bwd:
                 b = fwd + t
-                chunk = ring(t - bwd)
+                chunk = ring(q, t - bwd)
                 rs_wait(b - 1, q, chunk)
                 v = rs_recv[b - 1, q].astype(F32) + own[q, chunk]
                 rs_send[b, q] = v.astype(BF16)
-                rs_start(b, q, chunk, prev_dev)
+                rs_start(b, q, chunk, ring_dev(q, -1))
 
         each(pieces, onward)
 
@@ -502,20 +551,23 @@
     mean = jnp.sum(jnp.where(hit, power, 0.0), axis=1, keepdims=True) / float(width)
     factor = lax.rsqrt(mean + 1e-05)
 
-    def ag_start(slot, q, chunk, target):
+    legs = (1, 2, 3, 4, -1, -2, -3)
+
+    def ag_start(leg, q, chunk, step):
         def go(r, kind):
             copy_to(
                 hbuf.at[q, chunk, r],
                 hbuf.at[q, chunk, r],
                 size_send.at[2 + kind],
-                ag_sem.at[slot, q],
-                target,
+                ag_sem.at[legs.index(leg), q],
+                ring_dev(q, step),
             ).start()
 
         sized(chunk, go)
 
-    def ag_wait(slot, q, chunk):
-        sized(chunk, lambda r, kind: wait_bytes(hbuf.at[q, chunk, r], ag_sem.at[slot, q]))
+    def ag_wait(leg, q):
+        chunk = ring(q, -leg)
+        sized(chunk, lambda r, kind: wait_bytes(hbuf.at[q, chunk, r], ag_sem.at[legs.index(leg), q]))
 
     def finish(q):
         rs_wait(fwd - 1, q, m)
@@ -525,61 +577,47 @@
         ga = v[:, :LANES]
         up_half = v[:, LANES:]
         hbuf[q, m] = (ga / (1.0 + jnp.exp(-ga)) * up_half).astype(BF16)
-        ag_start(0, q, m, next_dev)
-        ag_start(fwd, q, m, prev_dev)
+        for leg in (2, -2, 1, -1):
+            ag_start(leg, q, m, leg)
 
     each(pieces, finish)
 
-    for t in range(1, fwd):
-
-        def relay(q, t=t):
-            ag_wait(t - 1, q, ring(-t))
-            ag_start(t, q, ring(-t), next_dev)
-            if t < bwd:
-                b = fwd + t
-                ag_wait(b - 1, q, ring(t))
-                ag_start(b, q, ring(t), prev_dev)
-
-        each(pieces, relay)
-
-    def arrived(q):
-        ag_wait(fwd - 1, q, ring(-fwd))
-        ag_wait(MSPLIT - 2, q, ring(bwd))
-
-    each(pieces, arrived)
+    def relay(q):
+        ag_wait(2, q)
+        ag_start(4, q, ring(q, -2), 2)
+        ag_start(3, q, ring(q, -2), 1)
+        ag_wait(-2, q)
+        ag_start(-3, q, ring(q, 2), -1)
+
+    each(pieces, relay)
 
     loads[4].wait()
     col_iota = lax.broadcasted_iota(jnp.int32, (batch, rows), 1).astype(F32)
     row_iota = lax.broadcasted_iota(jnp.int32, (rows, LANES), 0)
     filled = lax.rem(row_iota, 2 * pad) < pad + short
-    spreads = []
     for e in range(RESIDENT):
-        hc = jnp.concatenate(
-            [
-                jnp.where(
-                    filled,
-                    hbuf[q, e * quarters : (e + 1) * quarters].astype(F32).reshape(rows, LANES),
-                    0.0,
-                ).astype(BF16)
-                for q in range(pieces)
-            ],
-            axis=1,
-        )
-        pick = jnp.where(col_iota == cols_i[e], 1.0, 0.0).astype(BF16)
-        spreads.append(nn_dot(pick, hc).astype(BF16))
-    tile = 256
-    for c in range(bw // tile):
-        cols = slice(c * tile, (c + 1) * tile)
-        total = jnp.zeros((batch, tile), F32)
+        picks[e] = jnp.where(col_iota == cols_i[e], 1.0, 0.0).astype(BF16)
+    acc[...] = jnp.zeros_like(acc)
+
+    def down(q):
+        for leg in (1, -1, 3, -3, 4):
+            ag_wait(leg, q)
+        units = pl.ds(pl.multiple_of(q * LANES, LANES), LANES)
         for e in range(RESIDENT):
-            total = total + info[:, e : e + 1] * nn_dot(spreads[e], dwbuf[e, :, cols])
-        kout[:, :, cols] = total.astype(BF16).reshape(hsplit, 8, tile)
-
-    def ffn_send(i):
-        j = lax.rem(h + i, hsplit)
+            hc = hbuf[q, e * quarters : (e + 1) * quarters].astype(F32).reshape(rows, LANES)
+            hc = jnp.where(filled, hc, 0.0).astype(BF16)
+            spread = nn_dot(picks[e], hc).astype(BF16)
+            acc[e] += nn_dot(spread, dwbuf[e, units, :])
+
+    each(pieces, down)
+    total = info[:, 0:1] * acc[0]
+    for e in range(1, RESIDENT):
+        total = total + info[:, e : e + 1] * acc[e]
+    kout[...] = total.astype(BF16).reshape(hsplit, 8, bw)
+
+    for step in patch_steps:
+        j = patch_peer(step)
         copy_to(kout.at[j], kin.at[h], one_send.at[9], one_recv.at[7], m * hsplit + j).start()
-
-    each(hsplit, ffn_send, 1)
     kin[h] = kout[h]
     wait_bytes(kin.at[pl.ds(0, hsplit - 1)], one_recv.at[7])
     ffn = kin[0].astype(F32)
@@ -615,7 +653,7 @@
         @pl.when(lax.rem(m, 2) == parity)
         def _(parity=parity):
             rs_even = MSPLIT // 2 - (1 - parity)
-            ag_steps = list(range(fwd)) + list(range(bwd))
+            ag_steps = (0, 0, 0, 0, -2, -2, 2)
             ag_even = sum((parity + step) % 2 == 0 for step in ag_steps)
             wait_bytes(rs_send.at[pl.ds(0, rs_even)], size_send.at[0])
             wait_bytes(rs_send.at[pl.ds(0, hops - rs_even), :, pl.ds(0, short)], size_send.at[1])
@@ -623,12 +661,26 @@
             wait_bytes(hbuf.at[:, pl.ds(0, hops - ag_even), pl.ds(0, short)], size_send.at[3])
 
     wait_bytes(kin.at[pl.ds(0, hsplit - 1)], one_send.at[9])
+    wait_bytes(route_all.at[pl.ds(0, hsplit - 1)], one_send.at[10])
+
+    @pl.when(k != gatherer)
+    def _():
+        wait_bytes(sblk, st_send.at[0])
+        wait_bytes(meta_out, me_send.at[0])
+
+    @pl.when((k == gatherer) & (z == h))
+    def _():
+        wait_bytes(pst.at[pl.ds(0, MSPLIT - 1)], st_send.at[1])
+        wait_bytes(route_all.at[pl.ds(0, MSPLIT - 1)], me_send.at[1])
+
+    @pl.when((k == gatherer) & (z != h))
+    def _():
+        wait_bytes(pst, st_send.at[1])
+        wait_bytes(route_all.at[pl.ds(0, MSPLIT)], me_send.at[1])
 
     def drain(j):
         @pl.when(j * hsplit + z != me)
         def _():
-            wait_bytes(sblk.at[j], st_send.at[j])
-            wait_bytes(meta_out, me_send.at[j])
             wait_bytes(lbuf.at[j], l_recv.at[j])
 
         @pl.when(h * PLANE + j != me)
@@ -720,28 +772,36 @@
         vmem(1, kv),
         vmem(1, kv),
         vmem(width // LANES, LANES, dtype=F32),
+        pltpu.SMEM((1,), jnp.int32),
+        pltpu.SMEM((1, 2), jnp.int32),
+        pltpu.SMEM((1, 2), F32),
+        vmem(MSPLIT, PLANE, 8, LANES),
+        vmem(PLANE, 1, LANES, dtype=F32),
+        vmem(8, LANES, dtype=F32),
+        vmem(hsplit, 8, LANES, dtype=F32),
+        vmem(RESIDENT, n, bw, dtype=F32),
+        vmem(RESIDENT, n, quarters * pad),
+        pltpu.SemaphoreType.DMA((14,)),
         pltpu.SemaphoreType.DMA((11,)),
-        pltpu.SemaphoreType.DMA((10,)),
-        pltpu.SemaphoreType.DMA((8,)),
+        pltpu.SemaphoreType.DMA((9,)),
         pltpu.SemaphoreType.DMA((planes,)),
         pltpu.SemaphoreType.REGULAR((4,)),
         pltpu.SemaphoreType.DMA((4,)),
-        pltpu.SemaphoreType.DMA((MSPLIT,)),
-        pltpu.SemaphoreType.DMA((PLANE,)),
-        pltpu.SemaphoreType.DMA((MSPLIT,)),
-        pltpu.SemaphoreType.DMA((PLANE,)),
+        pltpu.SemaphoreType.DMA((2,)),
+        pltpu.SemaphoreType.DMA((2,)),
+        pltpu.SemaphoreType.DMA((2,)),
+        pltpu.SemaphoreType.DMA((2,)),
         pltpu.SemaphoreType.DMA((hops, pieces)),
         pltpu.SemaphoreType.DMA((hops, pieces)),
         pltpu.SemaphoreType.DMA((PLANE,)),
         pltpu.SemaphoreType.DMA((MSPLIT,)),
     ]
-    smem = pl.BlockSpec(memory_space=pltpu.SMEM)
     local = pl.BlockSpec(memory_space=pltpu.VMEM)
     anywhere = pl.BlockSpec(memory_space=pl.ANY)
     return pl.pallas_call(
         functools.partial(layer_kernel, cfg),
         out_shape=jax.ShapeDtypeStruct((1, width), F32),
-        in_specs=[smem] * 3 + [anywhere] * 11,
+        in_specs=[anywhere] * 14,
         out_specs=local,
         scratch_shapes=scratch,
         compiler_params=pltpu.CompilerParams(

time: 104 us -> 98.5 us (0.947)
  Pallas kernels: 102 us -> 96.3 us
    pallas_call x1, Pallas kernels: 102 us -> 96.3 us  [on_device(): pl.pallas_call(functools.partial(layer_kernel, cfg), out_shape=jax.ShapeD...]
where the time goes in v3:
time: 98.5 us; the launch traced here: 98.3 us
  Pallas kernels  96.3 us (98%)
  other arithmetic  1.4 us (1%)
    pallas_call x1, Pallas kernels, on_device(): pl.pallas_call(functools.partial(layer_kernel, cfg), out_shape=jax.ShapeD...  96.3 us

profile of v3, /device:TPU:33, one launch (start us, length us, event | category | flops | bytes accessed | tf_op | source)
XLA Modules:
  0.0 98.3 jit_solution(14512245859755408350)
XLA Ops:
  0.7 96.3 %layer.1 = f32[1,8192]{1,0:T(1,128)} custom-call(s32[1]{0:T(128)S(6)} %copy.15.lengths_in, s32[1,2]{1,0:T(1,128)} %ids_in.1, f32[1,2]{1,0:T(1,128)} %scores_in.1, bf16[1,8192]{1,0:T(2,128)(2,1)} %stream_in.1, bf16[1,8192]{1,0:T(2,128)(2,1)} %query.1, bf16[1,1024]{1,0:T(2,128)(2,1)} %key_new.1, bf16[1,1024]{1,0:T(2,128)(2,1)} %value_new.1, ...), custom_call_target="tpu_custom_call" | custom-call | tf_op jit(solution)/shard_map/layer/pallas_call | solution.py:801
  96.9 1.4 %convert_element_type.3 = bf16[1,8192]{1,0:T(2,128)(2,1)} convert(f32[1,8192]{1,0:T(1,128)} %layer.1) | non-fusion elementwise | flops 8192 | bytes 49152 | tf_op jit(solution)/shard_map/convert_element_type | solution.py:826

commit v4 on v3

--- a/solution.py
+++ b/solution.py
@@ -270,10 +270,6 @@
     for step in plane_steps:
         signal(tok.at[3], z * PLANE + peer(*step))
 
-    pl.semaphore_wait(tok.at[0], 2)
-    for step in (2, -2):
-        signal(tok.at[1], up(step) * PLANE + k)
-
     for load in small[4:]:
         load.wait()
     for j in range(width // LANES):
@@ -322,6 +318,10 @@
             one_recv.at[1],
             z * PLANE + j,
         ).start()
+
+    pl.semaphore_wait(tok.at[0], 2)
+    for step in (2, -2):
+        signal(tok.at[1], up(step) * PLANE + k)
 
     wait_bytes(abuf.at[0, pl.ds(0, PLANE - 1)], one_recv.at[0])
     pl.semaphore_wait(tok.at[1], 2)

time: 98.5 us -> 97.3 us (0.988)
  Pallas kernels: 96.3 us -> 95 us
    pallas_call x1, Pallas kernels: 96.3 us -> 95 us  [on_device(): pl.pallas_call(functools.partial(layer_kernel, cfg), out_shape=jax.ShapeD...]
where the time goes in v4:
time: 97.3 us; the launch traced here: 97.1 us
  Pallas kernels  95 us (98%)
  other arithmetic  1.4 us (1%)
    pallas_call x1, Pallas kernels, on_device(): pl.pallas_call(functools.partial(layer_kernel, cfg), out_shape=jax.ShapeD...  95 us

profile of v4, /device:TPU:33, one launch (start us, length us, event | category | flops | bytes accessed | tf_op | source)
XLA Modules:
  0.0 97.1 jit_solution(4011948182158033371)
XLA Ops:
  0.7 95.0 %layer.1 = f32[1,8192]{1,0:T(1,128)} custom-call(s32[1]{0:T(128)S(6)} %copy.15.lengths_in, s32[1,2]{1,0:T(1,128)} %ids_in.1, f32[1,2]{1,0:T(1,128)} %scores_in.1, bf16[1,8192]{1,0:T(2,128)(2,1)} %stream_in.1, bf16[1,8192]{1,0:T(2,128)(2,1)} %query.1, bf16[1,1024]{1,0:T(2,128)(2,1)} %key_new.1, bf16[1,1024]{1,0:T(2,128)(2,1)} %value_new.1, ...), custom_call_target="tpu_custom_call" | custom-call | tf_op jit(solution)/shard_map/layer/pallas_call | solution.py:801
  95.7 1.4 %convert_element_type.3 = bf16[1,8192]{1,0:T(2,128)(2,1)} convert(f32[1,8192]{1,0:T(1,128)} %layer.1) | non-fusion elementwise | flops 8192 | bytes 49152 | tf_op jit(solution)/shard_map/convert_element_type | solution.py:826

commit v5 on v4

--- a/solution.py
+++ b/solution.py
@@ -115,6 +115,7 @@
     route_all,
     acc,
     picks,
+    wvm,
     loc_sem,
     one_send,
     one_recv,
@@ -181,9 +182,7 @@
         pltpu.make_async_copy(gate_weight, gbuf, loc_sem.at[2]),
         pltpu.make_async_copy(up_weight, ubuf, loc_sem.at[3]),
         pltpu.make_async_copy(down_weight, dwbuf, loc_sem.at[4]),
-        pltpu.make_async_copy(
-            out_weight.at[:, pl.ds(pl.multiple_of(k * bw, bw), bw)], wbuf.at[k], loc_sem.at[5]
-        ),
+        pltpu.make_async_copy(out_weight, wvm, loc_sem.at[5]),
     ]
     for load in loads[:2]:
         load.start()
@@ -212,7 +211,8 @@
 
     each(PLANE, greet, 1)
 
-    for load in loads[2:]:
+    loads[5].start()
+    for load in loads[2:5]:
         load.start()
 
     for load in small[:4]:
@@ -308,11 +308,12 @@
             pst[j, k] = sblk[j]
         pme[k] = meta_out[...]
 
+    loads[5].wait()
     pl.semaphore_wait(tok.at[3], PLANE - 1)
-    for step in plane_steps:
+    for step in sorted(plane_steps, key=lambda step: step[0] == 2):
         j = peer(*step)
         copy_to(
-            out_weight.at[:, pl.ds(pl.multiple_of(j * bw, bw), bw)],
+            wvm.at[:, pl.ds(pl.multiple_of(j * bw, bw), bw)],
             wbuf.at[k],
             one_send.at[1],
             one_recv.at[1],
@@ -383,7 +384,7 @@
 
     each(planes, z_wait, 1)
 
-    loads[5].wait()
+    wbuf[k] = wvm[:, pl.ds(pl.multiple_of(k * bw, bw), bw)]
     wait_bytes(wbuf.at[pl.ds(0, PLANE - 1)], one_recv.at[1])
 
     af[...] = abuf[...].reshape(batch * 8, LANES).astype(F32)
@@ -781,6 +782,7 @@
         vmem(hsplit, 8, LANES, dtype=F32),
         vmem(RESIDENT, n, bw, dtype=F32),
         vmem(RESIDENT, n, quarters * pad),
+        vmem(cols, width),
         pltpu.SemaphoreType.DMA((14,)),
         pltpu.SemaphoreType.DMA((11,)),
         pltpu.SemaphoreType.DMA((9,)),

time: 97.3 us -> 96.6 us (level)
  no operation moved by 1% of the time
where the time goes in v5:
time: 96.6 us; the launch traced here: 96.4 us
  Pallas kernels  94.3 us (98%)
  other arithmetic  1.4 us (1%)
    pallas_call x1, Pallas kernels, on_device(): pl.pallas_call(functools.partial(layer_kernel, cfg), out_shape=jax.ShapeD...  94.3 us

profile of v5, /device:TPU:33, one launch (start us, length us, event | category | flops | bytes accessed | tf_op | source)
XLA Modules:
  0.0 96.4 jit_solution(5499734886163335643)
XLA Ops:
  0.7 94.3 %layer.1 = f32[1,8192]{1,0:T(1,128)} custom-call(s32[1]{0:T(128)S(6)} %copy.15.lengths_in, s32[1,2]{1,0:T(1,128)} %ids_in.1, f32[1,2]{1,0:T(1,128)} %scores_in.1, bf16[1,8192]{1,0:T(2,128)(2,1)} %stream_in.1, bf16[1,8192]{1,0:T(2,128)(2,1)} %query.1, bf16[1,1024]{1,0:T(2,128)(2,1)} %key_new.1, bf16[1,1024]{1,0:T(2,128)(2,1)} %value_new.1, ...), custom_call_target="tpu_custom_call" | custom-call | tf_op jit(solution)/shard_map/layer/pallas_call | solution.py:803
  95.0 1.4 %convert_element_type.3 = bf16[1,8192]{1,0:T(2,128)(2,1)} convert(f32[1,8192]{1,0:T(1,128)} %layer.1) | non-fusion elementwise | flops 8192 | bytes 49152 | tf_op jit(solution)/shard_map/convert_element_type | solution.py:828

commit v6 on v5

--- a/solution.py
+++ b/solution.py
@@ -430,7 +430,9 @@
         target = m * hsplit + patch_peer(step)
         copy_to(yblk, xbuf.at[h], one_send.at[5], one_recv.at[5], target).start()
     ssq = jnp.sum(resid * resid, axis=1, keepdims=True)
-    meta_blk[...] = jnp.broadcast_to(ssq, (8, LANES))
+    row8 = lax.broadcasted_iota(jnp.int32, (8, LANES), 0)
+    lane8 = lax.broadcasted_iota(jnp.int32, (8, LANES), 1)
+    meta_blk[...] = jnp.sum(jnp.where(lane8 == h * 8 + row8, ssq, 0.0), axis=0, keepdims=True)
     meta_all[h] = meta_blk[...]
     for step in patch_steps:
         target = m * hsplit + patch_peer(step)
@@ -515,7 +517,10 @@
     each(pieces, first)
 
     wait_bytes(meta_all.at[pl.ds(0, hsplit - 1)], one_recv.at[4])
-    ssq_row[...] = meta_all[...].reshape(batch, LANES).T[0:1]
+    block_sum = meta_all[0]
+    for j in range(1, hsplit):
+        block_sum = block_sum + meta_all[j]
+    ssq_row[...] = block_sum
     ssq_all[m] = ssq_row[...]
 
     def ssq_send(i):
@@ -751,8 +756,8 @@
         vmem(PLANE, 8, LANES),
         vmem(1, LANES, dtype=F32),
         vmem(PLANE, 1, LANES, dtype=F32),
-        vmem(8, LANES, dtype=F32),
-        vmem(hsplit, 8, LANES, dtype=F32),
+        vmem(1, LANES, dtype=F32),
+        vmem(hsplit, 1, LANES, dtype=F32),
         vmem(8, bw, dtype=F32),
         vmem(8, bw),
         vmem(hsplit, 8, bw),

time: 96.6 us -> 96.5 us (level)
  no operation moved by 1% of the time
where the time goes in v6:
time: 96.5 us; the launch traced here: 96.4 us
  Pallas kernels  94.3 us (98%)
  other arithmetic  1.4 us (1%)
    pallas_call x1, Pallas kernels, on_device(): pl.pallas_call(functools.partial(layer_kernel, cfg), out_shape=jax.ShapeD...  94.3 us

profile of v6, /device:TPU:33, one launch (start us, length us, event | category | flops | bytes accessed | tf_op | source)
XLA Modules:
  0.0 96.4 jit_solution(433803508494756866)
XLA Ops:
  0.7 94.3 %layer.1 = f32[1,8192]{1,0:T(1,128)} custom-call(s32[1]{0:T(128)S(6)} %copy.15.lengths_in, s32[1,2]{1,0:T(1,128)} %ids_in.1, f32[1,2]{1,0:T(1,128)} %scores_in.1, bf16[1,8192]{1,0:T(2,128)(2,1)} %stream_in.1, bf16[1,8192]{1,0:T(2,128)(2,1)} %query.1, bf16[1,1024]{1,0:T(2,128)(2,1)} %key_new.1, bf16[1,1024]{1,0:T(2,128)(2,1)} %value_new.1, ...), custom_call_target="tpu_custom_call" | custom-call | tf_op jit(solution)/shard_map/layer/pallas_call | solution.py:808
  95.0 1.4 %convert_element_type.3 = bf16[1,8192]{1,0:T(2,128)(2,1)} convert(f32[1,8192]{1,0:T(1,128)} %layer.1) | non-fusion elementwise | flops 8192 | bytes 49152 | tf_op jit(solution)/shard_map/convert_element_type | solution.py:833
